TPU v7x, 128 devices: a whole 4x4x4 slice. The times are simulated.
128 devices in a mesh: wide: 32 (over z, x, core), narrow: 4 (over y).
Axes of the slice: x: 4, y: 4, z: 4, core: 2. Of those that a mesh axis runs over, the one named last changes fastest.
Arguments:
- dens_tiles: bfloat16 [2048, 3, 128, 128], P(('wide', 'narrow')), may hold values from -6 to 6
- tile_dest: int32 [2048, 2], P(('wide', 'narrow')), may hold values from 0 to 31, all different within a row; in each aligned block of 16 rows (0 to 15, 16 to 31, ...) at most 2 rows name the same one
- tile_place: int32 [2048, 2], P(('wide', 'narrow')), may hold values from 0 to 49
- tile_rows: int32 [2048], P(('wide', 'narrow')), may hold values from 0 to 3
- tile_cols: int32 [2048], P(('wide', 'narrow')), may hold values from 0 to 31
- ao_values: bfloat16 [64, 640, 1280], P('wide'), may hold values from -0.25 to 0.25
- point_count: int32 [64], P('wide'), may hold values from 1 to 1280, 51200 in all
- weights: float32 [64, 1280], P('wide'), may hold values from 0.05 to 1
- kernel_first: float32 [64, 1280], P('wide'), may hold values from -1.5 to -0.3
- kernel_second: float32 [64, 1280], P('wide'), may hold values from 0.2 to 2
- occ_coef: bfloat16 [16384, 512], P('wide'), may hold values from -0.3125 to 0.3125
- vir_coef: bfloat16 [16384, 1024], P('narrow'), may hold values from -0.3125 to 0.3125
Outputs:
- response: float32 [3, 512, 1024], P(None, 'wide', 'narrow')
Inputs may be any that keep to these rules, and one draw needn't show every extreme that they name: `tile_dest`: among the routes of one device's 16 tiles, no wide index is named more than 2 times, and some device names some index exactly 2 times; the 2 indices of one tile differ. `point_count`: the counts of all batches sum to 51200.
All inputs are finite; a program needn't handle non-finite values. No bound on the sum of `point_count` on one device may be relied on, other than what follows from the above.
Results may differ from a plain program's by a relative error of at most 0.0074.
Values may be sent and summed in bfloat16 or wider, within the bound.
A program may use at most 128 MiB of HBM per device.

v0:
```python
import jax
import jax.numpy as jnp
from jax import lax
from jax.sharding import PartitionSpec as P

NOCC = 512
NVIR = 1024
BLK = 128
KB = 5
FIELDS = 3
TOP = 2
NBAT = 2


def copy_for_each(array, axis):
    count = lax.axis_size(axis)
    return lax.all_to_all(
        jnp.broadcast_to(array[None], (count, *array.shape)), axis, 0, 0, tiled=True
    )


def over_copies(array, axis):
    everything = copy_for_each(array, axis)
    return jnp.sum(everything, axis=0)


def in_blocks(array, dim, count):
    lengths = array.shape
    parts = array.reshape(*lengths[:dim], count, lengths[dim] // count, *lengths[dim + 1 :])
    return jnp.moveaxis(parts, dim, 0)


def sum_at_owner(array, axis, dim):
    count = lax.axis_size(axis)
    parts = lax.all_to_all(in_blocks(array, dim, count), axis, 0, 0, tiled=True)
    return jnp.sum(parts.astype(jnp.float32), axis=0)


def field_potential(density, kernel_one, kernel_two, point_scale):
    dens_a = density[:, 0]
    dens_b = density[:, 1]
    dens_c = density[:, 2]
    stacked = jnp.stack(
        [
            kernel_one * dens_a + kernel_two * dens_b * dens_c,
            kernel_one * dens_b + kernel_two * dens_a * dens_c,
            kernel_one * dens_c + kernel_two * dens_a * dens_b,
        ],
        axis=1,
    )
    return stacked * point_scale[:, None, :]


def body(
    dens_tiles,
    tile_dest,
    tile_place,
    tile_rows,
    tile_cols,
    ao_values,
    point_count,
    weights,
    kernel_first,
    kernel_second,
    occ_coef,
    vir_coef,
):
    wide_count = lax.axis_size("wide")
    tile_count = dens_tiles.shape[0]
    bucket = max(2, 2 * tile_count * TOP // wide_count)
    batch_slots = NBAT * KB * KB
    tile_len = FIELDS * BLK * BLK
    ao_width = KB * BLK
    total_slots = wide_count * bucket
    flat_tiles = dens_tiles.reshape(tile_count, tile_len)
    targets = tile_dest.reshape(-1)
    slot_places = tile_place.reshape(-1)
    target_hot = (targets[:, None] == jnp.arange(wide_count)[None, :]).astype(jnp.int32)
    before = jnp.cumsum(target_hot, axis=0) - target_hot
    position = targets * bucket + jnp.sum(before * target_hot, axis=1)
    chosen = position[None, :] == jnp.arange(total_slots)[:, None]
    picker = chosen.reshape(total_slots, tile_count, TOP).any(axis=2).astype(jnp.bfloat16)
    outgoing = jnp.dot(picker, flat_tiles, preferred_element_type=jnp.float32).astype(jnp.bfloat16)
    out_place = jnp.where(
        chosen.any(axis=1), jnp.sum(jnp.where(chosen, slot_places[None, :], 0), axis=1), -1
    )
    incoming, in_place = (
        lax.all_to_all(
            outgoing.reshape(wide_count, bucket, tile_len),
            "wide",
            split_axis=0,
            concat_axis=0,
            tiled=True,
        ),
        lax.all_to_all(
            out_place.reshape(wide_count, bucket), "wide", split_axis=0, concat_axis=0, tiled=True
        ),
    )
    landing = (in_place.reshape(-1)[None, :] == jnp.arange(batch_slots)[:, None]).astype(
        jnp.bfloat16
    )
    land_grid = jnp.dot(
        landing, incoming.reshape(total_slots, tile_len), preferred_element_type=jnp.float32
    ).astype(jnp.bfloat16)
    dens_grid = (
        land_grid.reshape(NBAT, KB, KB, FIELDS, BLK, BLK)
        .transpose(0, 3, 1, 4, 2, 5)
        .reshape(NBAT, FIELDS, ao_width, ao_width)
    )
    mixed_rows = jnp.einsum(
        "bfmn,bnp->bfmp", dens_grid, ao_values, preferred_element_type=jnp.float32
    )
    partial_rho = jnp.sum(mixed_rows * ao_values[:, None], axis=2)
    density = over_copies(partial_rho, "narrow")
    inside = jnp.arange(ao_values.shape[2])[None, :] < point_count[:, None]
    point_scale = jnp.where(inside, weights, jnp.float32(0.0))
    potential = field_potential(density, kernel_first, kernel_second, point_scale)
    scaled = (ao_values[:, None] * potential[:, :, None, :]).astype(jnp.bfloat16)
    blocks = jnp.einsum("bfmp,bnp->bfmn", scaled, ao_values, preferred_element_type=jnp.float32)
    blocks = blocks.reshape(NBAT, FIELDS, KB, BLK, KB, BLK).transpose(0, 2, 4, 1, 3, 5)
    blocks = blocks.reshape(batch_slots, tile_len).astype(jnp.bfloat16)
    answers = jnp.dot(landing.T, blocks, preferred_element_type=jnp.float32).astype(jnp.bfloat16)
    returned = lax.all_to_all(
        answers.reshape(wide_count, bucket, tile_len),
        "wide",
        split_axis=0,
        concat_axis=0,
        tiled=True,
    )
    tile_potential = jnp.dot(
        picker.T, returned.reshape(total_slots, tile_len), preferred_element_type=jnp.float32
    ).astype(jnp.bfloat16)
    occ_sel = occ_coef.reshape(-1, BLK, occ_coef.shape[1])[tile_rows]
    vir_sel = vir_coef.reshape(-1, BLK, vir_coef.shape[1])[tile_cols].reshape(
        tile_count * BLK, vir_coef.shape[1]
    )
    left_half = jnp.einsum(
        "tao,tfab->fotb",
        occ_sel,
        tile_potential.reshape(tile_count, FIELDS, BLK, BLK),
        preferred_element_type=jnp.float32,
    ).astype(jnp.bfloat16)
    partial_value = jnp.dot(
        left_half.reshape(FIELDS * NOCC, tile_count * BLK),
        vir_sel,
        preferred_element_type=jnp.float32,
    ).reshape(FIELDS, NOCC, NVIR)
    by_columns = sum_at_owner(partial_value.astype(jnp.bfloat16), "narrow", 2)
    result = sum_at_owner(by_columns.astype(jnp.bfloat16), "wide", 1)
    return result


def solution(mesh):
    in_specs = (
        P(("wide", "narrow"), None, None, None),
        P(("wide", "narrow"), None),
        P(("wide", "narrow"), None),
        P(("wide", "narrow")),
        P(("wide", "narrow")),
        P("wide", None, None),
        P("wide"),
        P("wide", None),
        P("wide", None),
        P("wide", None),
        P("wide", None),
        P("narrow", None),
    )
    out_specs = P(None, "wide", "narrow")
    return jax.shard_map(body, mesh=mesh, in_specs=in_specs, out_specs=out_specs, check_vma=False)
```

profile of v0, /device:TPU:0, one launch (start us, length us, event | category | flops | bytes accessed | tf_op | source)
XLA Modules:
  0.0 398.8 jit_solution(3670598510941739345)
XLA Ops:
  0.0 0.8 copy.76
  3.0 8.3 %all-to-all-start = ((s32[32,1,2]{2,1,0:T(1,128)}), s32[32,1,2]{2,1,0:T(1,128)S(1)}, u32[]{:S(2)}, u32[]{:S(2)}) async-start(s32[32,1,2]{2,1,0:T(1,128)} %bitcast), calls=%async_computation | async-start | bytes 32768 | tf_op jit(solution)/shard_map/all_to_all | solution.py:95
  12.2 5.9 %convolution_convert_fusion.1 = bf16[64,49152]{1,0:T(8,128)(2,1)} fusion(pred[64,16]{0,1:T(8,128)(4,1)S(1)} %fusion.27, bf16[2,8,384,128]{3,2,1,0:T(8,128)(2,1)} %bitcast.109), kind=kOutput, calls=%fused_computation.3 | convolution fusion | flops 103809024 | bytes 7865344 | tf_op jit(solution)/shard_map/dot_general | solution.py:83
  18.1 9.1 %reshape.123 = bf16[32,2,49152]{2,1,0:T(2,128)(2,1)} reshape(bf16[64,49152]{1,0:T(8,128)(2,1)} %convolution_convert_fusion.1) | data formatting | bytes 12582912 | tf_op jit(solution)/shard_map/reshape | solution.py:89
  27.2 7.7 %all-to-all-start.1 = ((bf16[32,2,49152]{2,1,0:T(2,128)(2,1)}), bf16[32,2,49152]{2,1,0:T(2,128)(2,1)}, u32[]{:S(2)}, u32[]{:S(2)}) async-start(bf16[32,2,49152]{2,1,0:T(2,128)(2,1)} %reshape.123), calls=%async_computation.1 | async-start | bytes 12582912 | tf_op jit(solution)/shard_map/all_to_all | solution.py:88
  34.9 5.2 %convert_element_type.52 = f32[2,640,1280]{2,1,0:T(8,128)} convert(bf16[2,640,1280]{2,1,0:T(8,128)(2,1)} %param.17) | non-fusion elementwise | flops 1638400 | bytes 9830400 | tf_op jit(solution)/shard_map/convert_element_type | solution.py:118
  41.4 71.2 %all-to-all-done.1 = bf16[32,2,49152]{2,1,0:T(2,128)(2,1)} async-done(((bf16[32,2,49152]{2,1,0:T(2,128)(2,1)}), bf16[32,2,49152]{2,1,0:T(2,128)(2,1)}, u32[]{:S(2)}, u32[]{:S(2)}) %all-to-all-start.1) | async-done | bytes 6291488 | tf_op jit(solution)/shard_map/all_to_all | solution.py:88
  112.6 8.7 %reshape.124 = bf16[64,49152]{1,0:T(8,128)(2,1)} reshape(bf16[32,2,49152]{2,1,0:T(2,128)(2,1)} %all-to-all-done.1) | data formatting | bytes 12582912 | tf_op jit(solution)/shard_map/reshape | solution.py:103
  121.3 4.4 %convolution_convert_fusion.2 = bf16[50,49152]{1,0:T(8,128)(2,1)S(1)} fusion(bf16[64,49152]{1,0:T(8,128)(2,1)} %reshape.124, s32[64]{0:T(128)S(1)} %eq.60), kind=kOutput, calls=%fused_computation.4 | convolution fusion | flops 317033600 | bytes 11206912 | tf_op jit(solution)/shard_map/dot_general | solution.py:102
  125.6 1.5 copy.95
  127.7 7.7 %copy.106 = bf16[2,5,5,3,128,128]{5,2,4,1,3,0:T(8,128)(2,1)} copy(bf16[2,5,5,3,128,128]{5,4,3,2,1,0:T(8,128)(2,1)S(1)} %bitcast.103) | data formatting | bytes 9830400 | tf_op jit(solution)/shard_map/reshape | solution.py:106
  135.4 11.8 %reshape.126 = bf16[2,3,640,640]{3,2,1,0:T(8,128)(2,1)} reshape(bf16[2,3,5,128,5,128]{5,4,3,2,1,0:T(8,128)(2,1)} %bitcast.100) | data formatting | bytes 9830400 | tf_op jit(solution)/shard_map/reshape | solution.py:108
  147.3 11.7 %multiply_reduce_fusion = f32[2,3,1280]{2,1,0:T(4,128)S(1)} fusion(bf16[2,3,640,640]{3,2,1,0:T(8,128)(2,1)} %reshape.126, f32[2,640,1280]{2,1,0:T(8,128)} %convert_element_type.52, bf16[2,640,1280]{2,1,0:T(8,128)(2,1)} %param.17), kind=kOutput, calls=%fused_computation.7 | convolution fusion | flops 6301278720 | bytes 14776320 | tf_op jit(solution)/shard_map/bfmn,bnp->bfmp/dot_general | solution.py:110
  159.7 4.5 %all-to-all-start.2 = ((f32[4,2,3,1280]{3,1,2,0:T(2,128)}), f32[4,2,3,1280]{3,1,2,0:T(2,128)S(1)}, u32[]{:S(2)}, u32[]{:S(2)}) async-start(f32[4,2,3,1280]{3,1,2,0:T(2,128)} %broadcast_in_dim.48), calls=%async_computation.2 | async-start | bytes 245760 | tf_op jit(solution)/shard_map/all_to_all | solution.py:17
  164.2 5.9 %all-to-all-done.2 = f32[4,2,3,1280]{3,1,2,0:T(2,128)S(1)} async-done(((f32[4,2,3,1280]{3,1,2,0:T(2,128)}), f32[4,2,3,1280]{3,1,2,0:T(2,128)S(1)}, u32[]{:S(2)}, u32[]{:S(2)}) %all-to-all-start.2) | async-done | bytes 122912 | tf_op jit(solution)/shard_map/all_to_all | solution.py:17
  170.2 12.1 %fusion.11 = bf16[2,3,640,640]{3,2,1,0:T(8,128)(2,1)} fusion(bf16[2,640,1280]{2,1,0:T(8,128)(2,1)} %param.17, f32[2,3,1280]{2,1,0:T(4,128)S(1)} %copy.82, f32[2,640,1280]{2,1,0:T(8,128)} %convert_element_type.52), kind=kOutput, calls=%fused_computation.21 | convolution fusion | flops 6303744000 | bytes 14776320 | tf_op jit(solution)/shard_map/bfmp,bnp->bfmn/dot_general | solution.py:119
  182.3 11.6 %convert_element_type.57 = bf16[2,3,5,128,5,128]{5,4,3,2,1,0:T(8,128)(2,1)} reshape(bf16[2,3,640,640]{3,2,1,0:T(8,128)(2,1)} %fusion.11) | data formatting | bytes 9830400 | tf_op jit(solution)/shard_map/convert_element_type | solution.py:121
  193.9 6.8 %copy.83 = bf16[2,5,5,3,128,128]{5,4,3,2,1,0:T(8,128)(2,1)} copy(bf16[2,5,5,3,128,128]{5,2,4,1,3,0:T(8,128)(2,1)} %bitcast.101) | data formatting | bytes 9830400 | tf_op jit(solution)/shard_map/convert_element_type | solution.py:121
  200.7 7.9 %convert_element_type.59 = bf16[50,49152]{1,0:T(8,128)(2,1)} reshape(bf16[2,5,5,3,128,128]{5,4,3,2,1,0:T(8,128)(2,1)} %copy.83) | data formatting | bytes 9830400 | tf_op jit(solution)/shard_map/convert_element_type | solution.py:121
  208.6 7.1 %convolution_convert_fusion = bf16[64,49152]{1,0:T(8,128)(2,1)} fusion(bf16[50,49152]{1,0:T(8,128)(2,1)} %convert_element_type.59, s32[64]{0:T(128)S(1)} %eq.60), kind=kOutput, calls=%fused_computation.2 | convolution fusion | flops 317721728 | bytes 11206912 | tf_op jit(solution)/shard_map/dot_general | solution.py:122
  215.7 9.1 %reshape.127 = bf16[32,2,49152]{2,1,0:T(2,128)(2,1)} reshape(bf16[64,49152]{1,0:T(8,128)(2,1)} %convolution_convert_fusion) | data formatting | bytes 12582912 | tf_op jit(solution)/shard_map/reshape | solution.py:124
  224.7 5.3 %all-to-all-start.3 = ((bf16[32,2,49152]{2,1,0:T(2,128)(2,1)}), bf16[32,2,49152]{2,1,0:T(2,128)(2,1)}, u32[]{:S(2)}, u32[]{:S(2)}) async-start(bf16[32,2,49152]{2,1,0:T(2,128)(2,1)} %reshape.127), calls=%async_computation.3 | async-start | bytes 12582912 | tf_op jit(solution)/shard_map/all_to_all | solution.py:123
  230.1 6.1 %gather_fusion.1 = bf16[16,128,1024]{2,1,0:T(8,128)(2,1)} fusion(bf16[32,128,1024]{2,1,0:T(8,128)(2,1)} %bitcast.107, s32[1024]{0:T(1024)S(1)} %pad_clamp_fusion), kind=kCustom, calls=%fused_computation.1 | custom fusion | bytes 8388672 | tf_op jit(solution)/shard_map/gather | solution.py:134
  236.9 70.7 %all-to-all-done.3 = bf16[32,2,49152]{2,1,0:T(2,128)(2,1)} async-done(((bf16[32,2,49152]{2,1,0:T(2,128)(2,1)}), bf16[32,2,49152]{2,1,0:T(2,128)(2,1)}, u32[]{:S(2)}, u32[]{:S(2)}) %all-to-all-start.3) | async-done | bytes 6291488 | tf_op jit(solution)/shard_map/all_to_all | solution.py:123
  307.7 8.8 %reshape.128 = bf16[64,49152]{1,0:T(8,128)(2,1)} reshape(bf16[32,2,49152]{2,1,0:T(2,128)(2,1)} %all-to-all-done.3) | data formatting | bytes 12582912 | tf_op jit(solution)/shard_map/reshape | solution.py:131
  316.4 3.7 fusion.24
  320.1 1.5 copy.96
  321.7 12.7 %bitcast_convert_fusion = bf16[3,512,1024]{2,1,0:T(8,128)(2,1)} fusion(bf16[16,128,1024]{2,1,0:T(8,128)(2,1)} %gather_fusion.1, bf16[16,128,512]{2,1,0:T(8,128)(2,1)S(1)} %gather_fusion, bf16[16,3,128,128]{3,2,1,0:T(8,128)(2,1)} %bitcast.108), kind=kOutput, calls=%fused_computation.12 | convolution fusion | flops 7252475904 | bytes 11010048 | tf_op jit(solution)/shard_map/dot_general | solution.py:143
  334.4 2.2 copy.107
  336.6 36.9 %all_to_all.31 = bf16[4,3,512,256]{3,2,1,0:T(8,128)(2,1)} all-to-all(bf16[4,3,512,256]{3,2,1,0:T(8,128)(2,1)S(1)} %bitcast.104), channel_id=1, replica_groups=mesh['wide'=32,'narrow'=4] {'narrow'}, dimensions={0} | all-to-all | bytes 6291456 | tf_op jit(solution)/shard_map/all_to_all | solution.py:35
  373.5 2.5 reduce_sum.64
  376.1 22.0 %all_to_all.32 = bf16[32,3,16,256]{3,2,1,0:T(8,128)(2,1)S(1)} all-to-all(bf16[32,3,16,256]{3,2,1,0:T(8,128)(2,1)S(1)} %copy.87), channel_id=1, replica_groups=mesh['wide'=32,'narrow'=4] {'wide'}, dimensions={0} | all-to-all | bytes 1572864 | tf_op jit(solution)/shard_map/all_to_all | solution.py:35
  (48 shorter events, 7.3 us)
Async XLA Ops:
  0.0 236.2 %copy-start = (bf16[512,512]{1,0:T(8,128)(2,1)S(1)}, bf16[512,512]{1,0:T(8,128)(2,1)}, u32[]{:S(2)}) copy-start(bf16[512,512]{1,0:T(8,128)(2,1)} %param.22) | copy-start | bytes 1572868
  3.0 24.2 %all-to-all-start = ((s32[32,1,2]{2,1,0:T(1,128)}), s32[32,1,2]{2,1,0:T(1,128)S(1)}, u32[]{:S(2)}, u32[]{:S(2)}) async-start(s32[32,1,2]{2,1,0:T(1,128)} %bitcast), calls=%async_computation | async-start | bytes 32768 | tf_op jit(solution)/shard_map/all_to_all | solution.py:95
  27.2 85.4 %all-to-all-start.1 = ((bf16[32,2,49152]{2,1,0:T(2,128)(2,1)}), bf16[32,2,49152]{2,1,0:T(2,128)(2,1)}, u32[]{:S(2)}, u32[]{:S(2)}) async-start(bf16[32,2,49152]{2,1,0:T(2,128)(2,1)} %reshape.123), calls=%async_computation.1 | async-start | bytes 12582912 | tf_op jit(solution)/shard_map/all_to_all | solution.py:88
  147.2 16.9 %copy-start.3 = (f32[2,1280]{1,0:T(2,128)S(1)}, f32[2,1280]{1,0:T(2,128)}, u32[]{:S(2)}) copy-start(f32[2,1280]{1,0:T(2,128)} %param.19) | copy-start | bytes 30724
  147.2 16.9 %copy-start.4 = (s32[2]{0:T(128)S(1)}, s32[2]{0:T(128)}, u32[]{:S(2)}) copy-start(s32[2]{0:T(128)} %param.18) | copy-start | bytes 28
  147.2 22.9 %copy-start.1 = (f32[2,1280]{1,0:T(2,128)S(1)}, f32[2,1280]{1,0:T(2,128)}, u32[]{:S(2)}) copy-start(f32[2,1280]{1,0:T(2,128)} %param.21) | copy-start | bytes 30724
  147.2 22.9 %copy-start.2 = (f32[2,1280]{1,0:T(2,128)S(1)}, f32[2,1280]{1,0:T(2,128)}, u32[]{:S(2)}) copy-start(f32[2,1280]{1,0:T(2,128)} %param.20) | copy-start | bytes 30724
  159.7 10.4 %all-to-all-start.2 = ((f32[4,2,3,1280]{3,1,2,0:T(2,128)}), f32[4,2,3,1280]{3,1,2,0:T(2,128)S(1)}, u32[]{:S(2)}, u32[]{:S(2)}) async-start(f32[4,2,3,1280]{3,1,2,0:T(2,128)} %broadcast_in_dim.48), calls=%async_computation.2 | async-start | bytes 245760 | tf_op jit(solution)/shard_map/all_to_all | solution.py:17
  224.7 5.3 %copy-start.5 = (s32[16]{0:T(128)S(1)}, s32[16]{0:T(128)}, u32[]{:S(2)}) copy-start(s32[16]{0:T(128)} %param.16) | copy-start | bytes 196
  224.7 82.9 %all-to-all-start.3 = ((bf16[32,2,49152]{2,1,0:T(2,128)(2,1)}), bf16[32,2,49152]{2,1,0:T(2,128)(2,1)}, u32[]{:S(2)}, u32[]{:S(2)}) async-start(bf16[32,2,49152]{2,1,0:T(2,128)(2,1)} %reshape.127), calls=%async_computation.3 | async-start | bytes 12582912 | tf_op jit(solution)/shard_map/all_to_all | solution.py:123
  230.1 6.2 %copy-start.6 = (s32[16]{0:T(128)S(1)}, s32[16]{0:T(128)}, u32[]{:S(2)}) copy-start(s32[16]{0:T(128)} %param.15) | copy-start | bytes 196
where the time goes:
time: 402 us; the launch traced here: 399 us
  waiting for transfers between devices  148 us (37%)
  local copies, waits for them, and re-layouts  98 us (24%)
  blocking collectives  58.9 us (15%)
  matrix products  57.6 us (14%)
  starting transfers between devices  25.7 us (6%)
  other arithmetic  10.6 us (3%)
    all_to_all x1, waiting for transfers between devices, body(): lax.all_to_all(outgoing.reshape(wide_count, bucket, tile_len), 'wide', sp...  71.2 us
    all_to_all x1, waiting for transfers between devices, body(): lax.all_to_all(answers.reshape(wide_count, bucket, tile_len), 'wide', spl...  70.7 us
    all_to_all x2, blocking collectives, sum_at_owner(): parts = lax.all_to_all(in_blocks(array, dim, count), axis, 0, 0, tiled=True)  58.9 us
    convert_element_type x3, local copies, waits for them, and re-layouts, body(): blocks = blocks.reshape(batch_slots, tile_len).astype(jnp.bfloat16)  26.3 us
    dot_general x1, matrix products, body(): jnp.dot(left_half.reshape(FIELDS * NOCC, tile_count * BLK), vir_sel, pref...  12.7 us
    dot_general x1, matrix products, body(): jnp.einsum('bfmp,bnp->bfmn', scaled, ao_values, preferred_element_type=jn...  12.1 us
    reshape x1, local copies, waits for them, and re-layouts, body(): dens_grid = land_grid.reshape(NBAT, KB, KB, FIELDS, BLK, BLK).transpose(0...  11.8 us
    dot_general x1, matrix products, body(): jnp.einsum('bfmn,bnp->bfmp', dens_grid, ao_values, preferred_element_type...  11.7 us
  transfers between devices with their start and end apart: 4, of which 3 were waited for; matrix products, arithmetic and copies ran while one was open for 7% of the time, Pallas kernels for 0%

commit v1 on v0

v1 whole, which is shorter than its diff:
```python
import jax
import jax.numpy as jnp
from jax import lax
from jax.experimental import pallas as pl
from jax.experimental.pallas import tpu as pltpu
from jax.sharding import PartitionSpec as P

NOCC = 512
NVIR = 1024
BLK = 128
KB = 5
FIELDS = 3
NBAT = 2
PTS = 1280
SIDE = 4
NWIDE = 32
ROWS = FIELDS * BLK
MESH = pl.DeviceIdType.MESH
CHIPS = [(2, 2), (1, 1), (3, 3), (1, 3), (3, 1), (1, 2), (3, 2), (2, 1), (2, 3), (0, 2), (2, 0), (0, 1), (0, 3), (1, 0), (3, 0)]
OFFSETS = [(z, x, c) for z, x in CHIPS for c in range(2)] + [(0, 0, 1)]


def shifted(me, offset, sign=1):
    z, x, c = me // 8, (me // 2) % 4, me % 2
    z = (z + sign * offset[0] + 2 * SIDE) % SIDE
    x = (x + sign * offset[1] + 2 * SIDE) % SIDE
    c = (c + offset[2]) % 2
    return z * 8 + x * 2 + c


def number(offset):
    return offset[0] * 8 + offset[1] * 2 + offset[2]


def dispatch_kernel(
    sel_ref, meta_ref, tiles_ref, ao_ref, dens_ref, info_ref,
    outb, inb, acc, mine, parts,
    send_sem, recv_sem, meta_send, meta_recv, part_send, part_recv,
):
    me = lax.axis_index("wide")
    row = lax.axis_index("narrow")
    barrier = pltpu.get_barrier_semaphore()
    for offset in OFFSETS:
        pl.semaphore_signal(
            barrier, inc=1, device_id={"wide": shifted(me, offset)}, device_id_type=MESH
        )
    for step in range(1, SIDE):
        pl.semaphore_signal(
            barrier, inc=1, device_id={"narrow": (row + step) % SIDE}, device_id_type=MESH
        )

    def build(i, carry):
        outb[i] = tiles_ref[sel_ref[i]]
        return carry

    lax.fori_loop(0, 2 * NWIDE, build, 0)
    acc[...] = jnp.zeros_like(acc)
    pl.semaphore_wait(barrier, len(OFFSETS) + SIDE - 1)

    sent = []

    def send(src, dst, ssem, rsem, peer):
        copy = pltpu.make_async_remote_copy(
            src_ref=src, dst_ref=dst, send_sem=ssem, recv_sem=rsem,
            device_id={"wide": peer}, device_id_type=MESH,
        )
        copy.start()
        sent.append(copy)

    for offset in OFFSETS:
        peer, k = shifted(me, offset), number(offset)
        send(meta_ref.at[peer], info_ref.at[me], meta_send.at[k], meta_recv.at[k], peer)
    info_ref[me] = meta_ref[me]
    for offset in OFFSETS:
        peer, k = shifted(me, offset), number(offset)
        for j in range(2):
            send(
                outb.at[2 * peer + j], inb.at[2 * me + j], send_sem.at[k, j], recv_sem.at[k, j], peer
            )

    def use(tile, code):
        first, second = code % 16, (code // 16) % 16
        batch, valid = (code // 256) % 2, (code // 32768) % 2
        lives = [jnp.logical_and(valid == 1, batch == b) for b in range(NBAT)]
        for q in range(PTS // 256):
            cols = pl.ds(q * 256, 256)
            mixed = jnp.dot(tile, ao_ref[second, :, cols], preferred_element_type=jnp.float32)
            left = ao_ref[first, :, cols].astype(jnp.float32)
            part = jnp.sum(
                mixed.reshape(FIELDS, BLK // 8, 8, 256) * left.reshape(1, BLK // 8, 8, 256), axis=1
            )
            for b in range(NBAT):
                acc[b, :, :, cols] += jnp.where(lives[b], part, 0.0)

    def code_of(ref, source, j):
        return ref[source, 0:1, j : j + 1][0, 0]

    for j in range(2):
        use(outb[2 * me + j], code_of(meta_ref, me, j))

    for offset in OFFSETS:
        peer, k = shifted(me, offset), number(offset)
        pltpu.make_async_remote_copy(
            src_ref=meta_ref.at[0], dst_ref=info_ref.at[0], send_sem=meta_send.at[k],
            recv_sem=meta_recv.at[k], device_id={"wide": peer}, device_id_type=MESH,
        ).wait_recv()

    def take(offset):
        k, source = number(offset), shifted(me, offset, -1)
        for j in range(2):
            pltpu.make_async_remote_copy(
                src_ref=outb.at[0], dst_ref=inb.at[2 * source + j], send_sem=send_sem.at[k, j],
                recv_sem=recv_sem.at[k, j], device_id={"wide": source}, device_id_type=MESH,
            ).wait_recv()
            use(inb[2 * source + j], code_of(info_ref, source, j))

    take((0, 0, 1))

    def arrive(i, carry):
        chip = i // 2
        dz = sum(jnp.where(chip == n, z, 0) for n, (z, _) in enumerate(CHIPS))
        dx = sum(jnp.where(chip == n, x, 0) for n, (_, x) in enumerate(CHIPS))
        take((dz, dx, i % 2))
        return carry

    lax.fori_loop(0, 2 * len(CHIPS), arrive, 0)

    for b in range(NBAT):
        for f in range(FIELDS):
            mine[pl.ds(b * FIELDS + f, 1), :] = jnp.sum(acc[b, f], axis=0, keepdims=True)
    mine[pl.ds(6, 2), :] = jnp.zeros((2, PTS), jnp.float32)
    total = mine[...]
    swaps = []
    for step in range(1, SIDE):
        copy = pltpu.make_async_remote_copy(
            src_ref=mine, dst_ref=parts.at[step - 1], send_sem=part_send.at[step - 1],
            recv_sem=part_recv.at[step - 1], device_id={"narrow": (row + step) % SIDE},
            device_id_type=MESH,
        )
        copy.start()
        swaps.append(copy)
    for copy in sent:
        copy.wait_send()
    for step, copy in enumerate(swaps):
        copy.wait()
        total = total + parts[step]
    dens_ref[...] = total


def dispatch(sel, meta, tiles, ao):
    vmem, smem = pl.BlockSpec(memory_space=pltpu.VMEM), pl.BlockSpec(memory_space=pltpu.SMEM)
    dma = pltpu.SemaphoreType.DMA
    return pl.pallas_call(
        dispatch_kernel,
        out_shape=(
            jax.ShapeDtypeStruct((8, PTS), jnp.float32),
            jax.ShapeDtypeStruct((NWIDE, 8, BLK), jnp.int32),
        ),
        in_specs=[smem, vmem, vmem, vmem],
        out_specs=(vmem, vmem),
        scratch_shapes=[
            pltpu.VMEM((2 * NWIDE, ROWS, BLK), jnp.bfloat16),
            pltpu.VMEM((2 * NWIDE, ROWS, BLK), jnp.bfloat16),
            pltpu.VMEM((NBAT, FIELDS, 8, PTS), jnp.float32),
            pltpu.VMEM((8, PTS), jnp.float32),
            pltpu.VMEM((SIDE - 1, 8, PTS), jnp.float32),
            dma((NWIDE, 2)), dma((NWIDE, 2)),
            dma((NWIDE,)), dma((NWIDE,)), dma((SIDE - 1,)), dma((SIDE - 1,)),
        ],
        compiler_params=pltpu.CompilerParams(
            collective_id=0, has_side_effects=True, vmem_limit_bytes=30 * 2**20
        ),
        cost_estimate=pl.CostEstimate(
            flops=70_000_000_000, bytes_accessed=10_000_000, transcendentals=0
        ),
    )(sel, meta, tiles, ao)


def respond_kernel(
    code_ref, count_ref, dens_ref, weight_ref, first_ref, second_ref, ao_ref, occ_hbm, vir_hbm,
    out_ref, occ, vir, pot, scaled, answer, total, left, head, follow, occ_sem, vir_sem,
):
    load_occ = pltpu.make_async_copy(occ_hbm, occ, occ_sem)
    load_vir = pltpu.make_async_copy(vir_hbm, vir, vir_sem)
    load_occ.start()
    load_vir.start()

    lane = lax.broadcasted_iota(jnp.int32, (1, PTS), 1)
    for b in range(NBAT):
        scale = jnp.where(lane < count_ref[b], weight_ref[pl.ds(b, 1), :], 0.0)
        one, two = first_ref[pl.ds(b, 1), :], second_ref[pl.ds(b, 1), :]
        d = [dens_ref[pl.ds(b * FIELDS + f, 1), :] for f in range(FIELDS)]
        for f in range(FIELDS):
            p, q = d[(f + 1) % 3], d[(f + 2) % 3]
            pot[pl.ds(b * FIELDS + f, 1), :] = scale * (one * d[f] + two * p * q)

    def blocks(i, carry):
        b, f = i // FIELDS, i % FIELDS
        aos = ao_ref[pl.ds(b * KB, KB)].reshape(KB * BLK, PTS)
        scaled[...] = (aos.astype(jnp.float32) * pot[pl.ds(i, 1), :]).astype(jnp.bfloat16)
        part = lax.dot_general(
            scaled[...], aos, (((1,), (1,)), ((), ())), preferred_element_type=jnp.float32
        ).astype(jnp.bfloat16)
        for a in range(KB):
            for c in range(KB):
                answer[b * 25 + a * KB + c, :, pl.ds(pl.multiple_of(f * BLK, BLK), BLK)] = part[
                    a * BLK : (a + 1) * BLK, c * BLK : (c + 1) * BLK
                ]
        return carry

    lax.fori_loop(0, NBAT * FIELDS, blocks, 0)

    def clear(c, carry):
        head[c] = -1
        return carry

    lax.fori_loop(0, 32, clear, 0)

    def link(r, carry):
        code = code_ref[r]
        column = (code // 262144) % 32

        @pl.when((code // 32768) % 2 == 1)
        def _():
            follow[r] = head[column]
            head[column] = r

        return carry

    lax.fori_loop(0, 2 * NWIDE, link, 0)
    load_occ.wait()

    def column_sum(c, carry):
        total[...] = jnp.zeros_like(total)

        def add(r):
            code = code_ref[r]
            block = (r // 2) * 4 + (code // 65536) % 4
            total[...] += jnp.dot(
                occ[block], answer[(code // 512) % 64], preferred_element_type=jnp.float32
            )
            return follow[r]

        lax.while_loop(lambda r: r >= 0, add, head[c])
        for f in range(FIELDS):
            left[pl.ds(f * NOCC, NOCC), pl.ds(pl.multiple_of(c * BLK, BLK), BLK)] = total[
                :, f * BLK : (f + 1) * BLK
            ].astype(jnp.bfloat16)
        return carry

    lax.fori_loop(0, 32, column_sum, 0)
    load_vir.wait()

    def project(i, carry):
        q, f = i // FIELDS, i % FIELDS
        rows = pl.ds(pl.multiple_of(f * NOCC, NOCC), NOCC)
        out_ref[q, rows, :] = jnp.dot(
            left[rows, :], vir[:, pl.ds(pl.multiple_of(q * 256, 256), 256)],
            preferred_element_type=jnp.float32,
        ).astype(jnp.bfloat16)
        return carry

    lax.fori_loop(0, SIDE * FIELDS, project, 0)


def respond(codes, counts, dens, weights, first, second, ao, occ, vir):
    vmem, smem = pl.BlockSpec(memory_space=pltpu.VMEM), pl.BlockSpec(memory_space=pltpu.SMEM)
    hbm = pl.BlockSpec(memory_space=pl.ANY)
    return pl.pallas_call(
        respond_kernel,
        out_shape=jax.ShapeDtypeStruct((SIDE, FIELDS * NOCC, 256), jnp.bfloat16),
        in_specs=[smem, smem, vmem, vmem, vmem, vmem, vmem, hbm, hbm],
        out_specs=vmem,
        scratch_shapes=[
            pltpu.VMEM((128, NOCC, BLK), jnp.bfloat16),
            pltpu.VMEM((4096, NVIR), jnp.bfloat16),
            pltpu.VMEM((8, PTS), jnp.float32),
            pltpu.VMEM((KB * BLK, PTS), jnp.bfloat16),
            pltpu.VMEM((50, BLK, ROWS), jnp.bfloat16),
            pltpu.VMEM((NOCC, ROWS), jnp.float32),
            pltpu.VMEM((FIELDS * NOCC, 4096), jnp.bfloat16),
            pltpu.SMEM((32,), jnp.int32),
            pltpu.SMEM((64,), jnp.int32),
            pltpu.SemaphoreType.DMA,
            pltpu.SemaphoreType.DMA,
        ],
        compiler_params=pltpu.CompilerParams(vmem_limit_bytes=62 * 2**20),
        cost_estimate=pl.CostEstimate(
            flops=30_000_000_000, bytes_accessed=30_000_000, transcendentals=0
        ),
    )(codes, counts, dens, weights, first, second, ao, occ, vir)


def turn_kernel(occ_ref, out_ref):
    row = lax.axis_index("narrow")
    out_ref[...] = occ_ref[pl.ds(pl.multiple_of(row * BLK, BLK), BLK), :].T


def turned(occ):
    vmem = pl.BlockSpec(memory_space=pltpu.VMEM)
    return pl.pallas_call(
        turn_kernel, out_shape=jax.ShapeDtypeStruct((NOCC, BLK), occ.dtype), in_specs=[vmem],
        out_specs=vmem,
    )(occ)


def body(
    dens_tiles,
    tile_dest,
    tile_place,
    tile_rows,
    tile_cols,
    ao_values,
    point_count,
    weights,
    kernel_first,
    kernel_second,
    occ_coef,
    vir_coef,
):
    tile_count = dens_tiles.shape[0]
    block = turned(occ_coef)
    occ_all = lax.all_gather(block[None], ("wide", "narrow"), axis=0, tiled=True)

    targets = tile_dest.reshape(-1)
    routes = jnp.arange(targets.shape[0])
    earlier = (targets[:, None] == targets[None, :]) & (routes[:, None] > routes[None, :])
    position = targets * 2 + jnp.sum(earlier.astype(jnp.int32), axis=1)
    place = tile_place.reshape(-1)
    batch, slot = place // 25, place % 25
    code = (
        (batch * KB + slot // KB) + 16 * (batch * KB + slot % KB) + 256 * batch + 512 * place + 32768
        + 65536 * jnp.repeat(tile_rows, 2) + 262144 * jnp.repeat(tile_cols, 2)
    )
    chosen = position[None, :] == jnp.arange(2 * NWIDE)[:, None]
    sel = jnp.sum(jnp.where(chosen, routes[None, :] // 2, 0), axis=1)
    codes = jnp.sum(jnp.where(chosen, code[None, :], 0), axis=1)
    meta = jnp.broadcast_to(
        jnp.pad(codes.reshape(NWIDE, 1, 2), ((0, 0), (0, 0), (0, BLK - 2))), (NWIDE, 8, BLK)
    )

    ao = ao_values.reshape(NBAT * KB, BLK, PTS)
    dens, info = dispatch(sel, meta, dens_tiles.reshape(tile_count, ROWS, BLK), ao)
    partial = respond(
        info[:, 0, :2].reshape(-1), point_count, dens, weights, kernel_first, kernel_second, ao,
        occ_all, vir_coef,
    )

    parts = lax.all_to_all(
        partial.reshape(SIDE, FIELDS, NOCC, 256), "narrow", 0, 0, tiled=True
    )
    by_columns = jnp.sum(parts.astype(jnp.float32), axis=0).astype(jnp.bfloat16)
    split = jnp.moveaxis(by_columns.reshape(FIELDS, NWIDE, NOCC // NWIDE, 256), 1, 0)
    owned = lax.all_to_all(split, "wide", 0, 0, tiled=True)
    return jnp.sum(owned.astype(jnp.float32), axis=0)


def solution(mesh):
    in_specs = (
        P(("wide", "narrow"), None, None, None),
        P(("wide", "narrow"), None),
        P(("wide", "narrow"), None),
        P(("wide", "narrow")),
        P(("wide", "narrow")),
        P("wide", None, None),
        P("wide"),
        P("wide", None),
        P("wide", None),
        P("wide", None),
        P("wide", None),
        P("narrow", None),
    )
    out_specs = P(None, "wide", "narrow")
    return jax.shard_map(body, mesh=mesh, in_specs=in_specs, out_specs=out_specs, check_vma=False)
```

time: 402 us -> 270 us (0.67)
  Pallas kernels: 0 us -> 144 us
  waiting for transfers between devices: 148 us -> 35.6 us
  local copies, waits for them, and re-layouts: 98 us -> 7.8 us
  matrix products: 57.6 us -> 0 us
  starting transfers between devices: 25.7 us -> 0.01 us
  between operations: 0.24 us -> 13.5 us
  other arithmetic: 10.6 us -> 5.3 us
    all_to_all x4 -> x0, waiting for transfers between devices: 148 us -> none  [the longest x1 71.2 us: body(): lax.all_to_all(outgoing.reshape(wide_count, bucket, tile_len), 'wide', sp...]
    pallas_call x0 -> x3, Pallas kernels: none -> 144 us  [the longest x1 100 us: dispatch(): pl.pallas_call(dispatch_kernel, out_shape=(jax.ShapeDtypeStruct((8, PTS),...]
    dot_general x7 -> x0, matrix products: 57.6 us -> none  [the longest x1 12.7 us: body(): jnp.dot(left_half.reshape(FIELDS * NOCC, tile_count * BLK), vir_sel, pref...]
    reshape x7 -> x2, local copies, waits for them, and re-layouts: 57.3 us -> 0.2 us  [the longest x1 0.11 us: body(): codes.reshape(NWIDE, 1, 2)]
    all_gather x0 -> x1, waiting for transfers between devices: none -> 35.6 us  [body(): lax.all_gather(block[None], ('wide', 'narrow'), axis=0, tiled=True)]
    convert_element_type x3 -> x0, local copies, waits for them, and re-layouts: 26.3 us -> none  [body(): blocks = blocks.reshape(batch_slots, tile_len).astype(jnp.bfloat16)]
    all_to_all x4 -> x0, starting transfers between devices: 25.7 us -> none  [the longest x1 8.27 us: body(): lax.all_to_all(out_place.reshape(wide_count, bucket), 'wide', split_axis=...]
    gather x2 -> x0, local copies, waits for them, and re-layouts: 6.8 us -> none  [the longest x1 6.12 us: body(): vir_coef.reshape(-1, BLK, vir_coef.shape[1])[tile_cols]]
  transfers between devices with their start and end apart: 4 -> 1, of which waited for: 3 -> 1; matrix products, arithmetic and copies ran while one was open for 7% -> 2% of each run, Pallas kernels for 0% -> 37%
where the time goes in v1:
time: 270 us; the launch traced here: 269 us
  Pallas kernels  144 us (53%)
  blocking collectives  62.3 us (23%)
  waiting for transfers between devices  35.6 us (13%)
  between operations  13.5 us (5%)
  local copies, waits for them, and re-layouts  7.8 us (3%)
  other arithmetic  5.3 us (2%)
    pallas_call x1, Pallas kernels, dispatch(): pl.pallas_call(dispatch_kernel, out_shape=(jax.ShapeDtypeStruct((8, PTS),...  100 us
    all_to_all x1, blocking collectives, body(): lax.all_to_all(partial.reshape(SIDE, FIELDS, NOCC, 256), 'narrow', 0, 0,...  43.3 us
    pallas_call x1, Pallas kernels, respond(): pl.pallas_call(respond_kernel, out_shape=jax.ShapeDtypeStruct((SIDE, FIEL...  42.5 us
    all_gather x1, waiting for transfers between devices, body(): lax.all_gather(block[None], ('wide', 'narrow'), axis=0, tiled=True)  35.6 us
    all_to_all x1, blocking collectives, body(): owned = lax.all_to_all(split, 'wide', 0, 0, tiled=True)  18.9 us
  transfers between devices with their start and end apart: 1, of which 1 were waited for; matrix products, arithmetic and copies ran while one was open for 2% of the time, Pallas kernels for 37%

profile of v1, /device:TPU:0, one launch (start us, length us, event | category | flops | bytes accessed | tf_op | source)
XLA Modules:
  0.0 268.7 jit_solution(190471112773635067)
XLA Ops:
  6.5 1.8 shard_map.119
  8.3 0.7 sign_compare_fusion
  9.0 0.1 copy.35
  9.1 0.1 ne.92
  9.2 0.7 broadcast_divide_fusion
  9.9 0.1 copy.37
  10.0 0.1 div.29
  10.1 0.7 broadcast_multiply_fusion.1
  10.8 0.1 mul.94
  10.9 0.7 broadcast_multiply_fusion.2
  11.6 0.1 mul.91
  11.7 0.1 copy.36
  11.8 0.1 rem.42
  11.9 0.1 copy.38
  12.0 0.1 mul.88
  12.1 0.8 copy.34
  12.8 0.1 reshape.140
  12.9 0.2 convert_reduce_fusion.1
  13.2 0.1 select_reduce_fusion
  13.3 0.1 reshape.141
  13.4 1.9 copy-done
  15.3 1.4 copy-done.1
  16.7 100.0 %shard_map.118 = (f32[8,1280]{1,0:T(8,128)S(1)}, s32[32,8,128]{2,1,0:T(8,128)S(1)}) custom-call(s32[64]{0:T(128)S(1)} %get-tuple-element.10.sel_ref, s32[32,8,128]{2,1,0:T(8,128)S(1)} %broadcast_in_dim.46.meta_ref, bf16[16,384,128]{2,1,0:T(8,128)(2,1)S(1)} %bitcast.11, bf16[10,128,1280]{2,1,0:T(8,128)(2,1)S(1)} %bitcast.10), custom_call_target="tpu_custom_call" | custom-call | flops 70000001024 | bytes 10000000 | tf_op jit(solution)/shard_map/pallas_call | solution.py:153
  116.7 0.6 copy-done.2
  117.4 0.6 reshape_squeeze.3.code_ref
  118.0 35.6 %all-gather.3.cloned.1.call-done = bf16[65536,128]{1,0:T(8,128)(2,1)} async-done(((bf16[512,128]{1,0:T(8,128)(2,1)}), bf16[65536,128]{1,0:T(8,128)(2,1)}) %all-gather.3.cloned.1.call-update) | async-done | bytes 16777232 | tf_op jit(solution)/shard_map/all_gather | solution.py:323
  153.6 42.5 %shard_map.120 = bf16[4,1536,256]{2,1,0:T(8,128)(2,1)} custom-call(s32[64]{0:T(128)} %reshape_squeeze.3.code_ref, s32[2]{0:T(128)} %count_ref.1, f32[8,1280]{1,0:T(8,128)} %copy-done.2, f32[2,1280]{1,0:T(2,128)} %weight_ref.1, f32[2,1280]{1,0:T(2,128)} %first_ref.1, f32[2,1280]{1,0:T(2,128)} %second_ref.1, bf16[10,128,1280]{2,1,0:T(8,128)(2,1)} %bitcast.9, ...), custom_call_target="tpu_custom_call" | custom-call | flops 30000001024 | bytes 30000000 | tf_op jit(solution)/shard_map/pallas_call | solution.py:269
  196.1 43.3 %all_to_all.10 = bf16[4,3,512,256]{3,2,1,0:T(8,128)(2,1)S(1)} all-to-all(bf16[4,3,512,256]{3,2,1,0:T(8,128)(2,1)} %bitcast.12), channel_id=1, replica_groups=mesh['wide'=32,'narrow'=4] {'narrow'}, dimensions={0} | all-to-all | bytes 6291456 | tf_op jit(solution)/shard_map/all_to_all | solution.py:349
  239.4 1.6 reduce_sum.51
  241.0 1.2 copy.39
  242.2 18.9 %all_to_all.11 = bf16[32,3,16,256]{3,2,1,0:T(8,128)(2,1)S(1)} all-to-all(bf16[32,3,16,256]{3,2,1,0:T(8,128)(2,1)S(1)} %copy.39), channel_id=1, replica_groups=mesh['wide'=32,'narrow'=4] {'wide'}, dimensions={0} | all-to-all | bytes 1572864 | tf_op jit(solution)/shard_map/all_to_all | solution.py:354
  261.1 0.7 convert_reduce_fusion
  (12 shorter events, 0.3 us)
Async XLA Ops:
  6.5 147.1 %all-gather.3.cloned.1.call-start = ((), (), s32[]{:S(2)}) async-start(), calls=%async_computation.2 | async-start | bytes 16908288 | tf_op jit(solution)/shard_map/all_gather | solution.py:323
  13.4 1.9 copy-start
  15.3 1.4 copy-start.1
  116.7 0.6 copy-start.2
Sparse Core Ops, SparseCore 0:
  10.5 143.1 all-gather.2

commit v2 on v1

--- a/solution.py
+++ b/solution.py
@@ -15,8 +15,10 @@
 SIDE = 4
 NWIDE = 32
 ROWS = FIELDS * BLK
+HALF = FIELDS * NOCC // 2
 MESH = pl.DeviceIdType.MESH
 CHIPS = [(2, 2), (1, 1), (3, 3), (1, 3), (3, 1), (1, 2), (3, 2), (2, 1), (2, 3), (0, 2), (2, 0), (0, 1), (0, 3), (1, 0), (3, 0)]
+BLOCKS_AHEAD, OUT_AHEAD, TILES_AHEAD, ON_AHEAD = 11, 8, 6, 4
 OFFSETS = [(z, x, c) for z, x in CHIPS for c in range(2)] + [(0, 0, 1)]
 
 
@@ -33,9 +35,10 @@
 
 
 def dispatch_kernel(
-    sel_ref, meta_ref, tiles_ref, ao_ref, dens_ref, info_ref,
-    outb, inb, acc, mine, parts,
+    sel_ref, meta_ref, tiles_ref, ao_ref, occ_ref, dens_ref, info_ref, all_ref,
+    outb, inb, acc, mine, parts, block,
     send_sem, recv_sem, meta_send, meta_recv, part_send, part_recv,
+    own_sem, plane_send, plane_recv, side_send, side_recv, pass_send, pass_recv, pair_send, pair_recv,
 ):
     me = lax.axis_index("wide")
     row = lax.axis_index("narrow")
@@ -49,6 +52,10 @@
             barrier, inc=1, device_id={"narrow": (row + step) % SIDE}, device_id_type=MESH
         )
 
+    turned = occ_ref[pl.ds(pl.multiple_of(row * BLK, BLK), BLK), :].T
+    for w in range(NWIDE):
+        block[pl.ds((w % 2) * 256 + (w // 2) * 16, 16), :] = turned[w * 16 : (w + 1) * 16]
+
     def build(i, carry):
         outb[i] = tiles_ref[sel_ref[i]]
         return carry
@@ -71,12 +78,99 @@
         peer, k = shifted(me, offset), number(offset)
         send(meta_ref.at[peer], info_ref.at[me], meta_send.at[k], meta_recv.at[k], peer)
     info_ref[me] = meta_ref[me]
-    for offset in OFFSETS:
-        peer, k = shifted(me, offset), number(offset)
-        for j in range(2):
-            send(
-                outb.at[2 * peer + j], inb.at[2 * me + j], send_sem.at[k, j], recv_sem.at[k, j], peer
-            )
+
+    def step_of(k):
+        dz = sum(jnp.where(k == n + 1, z, 0) for n, (z, _) in enumerate(CHIPS))
+        dx = sum(jnp.where(k == n + 1, x, 0) for n, (_, x) in enumerate(CHIPS))
+        return dz, dx
+
+    def home_of(k):
+        return shifted(me, (*step_of(k), 0), -1)
+
+    def slot(k, c, j, peer, source):
+        return pltpu.make_async_remote_copy(
+            src_ref=outb.at[2 * peer + j], dst_ref=inb.at[2 * source + j],
+            send_sem=send_sem.at[2 * k + c, j], recv_sem=recv_sem.at[2 * k + c, j],
+            device_id={"wide": peer}, device_id_type=MESH,
+        )
+
+    def send_tiles(k):
+        dz, dx = step_of(k)
+        for c in range(2):
+            for j in range(2):
+                slot(k, c, j, shifted(me, (dz, dx, c)), me).start()
+
+    def place(home, y):
+        return all_ref.at[home * SIDE + (y + 2 * SIDE) % SIDE]
+
+    def plane(k, peer, home):
+        return pltpu.make_async_remote_copy(
+            src_ref=block, dst_ref=place(home, row), send_sem=plane_send.at[k],
+            recv_sem=plane_recv.at[k], device_id={"wide": peer}, device_id_type=MESH,
+        )
+
+    def send_block(k):
+        plane(k, shifted(me, (*step_of(k), 0)), me).start()
+
+    def spread(src, k, home, side, way):
+        return pltpu.make_async_remote_copy(
+            src_ref=src, dst_ref=place(home, row), send_sem=side_send.at[k, side],
+            recv_sem=side_recv.at[k, side], device_id={"narrow": (row + way + SIDE) % SIDE},
+            device_id_type=MESH,
+        )
+
+    def passed(k, home, y, way):
+        return pltpu.make_async_remote_copy(
+            src_ref=place(home, y), dst_ref=place(home, y), send_sem=pass_send.at[k],
+            recv_sem=pass_recv.at[k], device_id={"narrow": (row + way + SIDE) % SIDE},
+            device_id_type=MESH,
+        )
+
+    def paired(k, home):
+        four = all_ref.at[pl.ds(home * SIDE, SIDE)]
+        return pltpu.make_async_remote_copy(
+            src_ref=four, dst_ref=four, send_sem=pair_send.at[k], recv_sem=pair_recv.at[k],
+            device_id={"wide": shifted(me, (0, 0, 1))}, device_id_type=MESH,
+        )
+
+    def outward(k):
+        home = home_of(k)
+        plane(k, home, home).wait_recv()
+        for side, way in enumerate((1, -1)):
+            spread(place(home, row), k, home, side, way).start()
+
+    def onward(k):
+        home = home_of(k)
+        for side, way in enumerate((1, -1)):
+            pltpu.make_async_remote_copy(
+                src_ref=block, dst_ref=place(home, row - way), send_sem=side_send.at[k, side],
+                recv_sem=side_recv.at[k, side], device_id={"narrow": (row - way + SIDE) % SIDE},
+                device_id_type=MESH,
+            ).wait_recv()
+        way = 1 - 2 * (k % 2)
+        passed(k, home, row - way, way).start()
+
+    def across(k):
+        home = home_of(k)
+        passed(k, home, row + 2, 1).wait_recv()
+        paired(k, home).start()
+
+    def each(first, last, step):
+        def run(k, carry):
+            step(k)
+            return carry
+
+        lax.fori_loop(first, last, run, 0)
+
+    keep = pltpu.make_async_copy(block, place(me, row), own_sem)
+    keep.start()
+    for side, way in enumerate((1, -1)):
+        spread(block, 0, me, side, way).start()
+    pair = shifted(me, (0, 0, 1))
+    for j in range(2):
+        slot(0, 1, j, pair, me).start()
+    each(1, 1 + BLOCKS_AHEAD, send_block)
+    each(1, 1 + TILES_AHEAD, send_tiles)
 
     def use(tile, code):
         first, second = code % 16, (code // 16) % 16
@@ -105,25 +199,28 @@
             recv_sem=meta_recv.at[k], device_id={"wide": peer}, device_id_type=MESH,
         ).wait_recv()
 
-    def take(offset):
-        k, source = number(offset), shifted(me, offset, -1)
+    def take(k, c, source):
         for j in range(2):
-            pltpu.make_async_remote_copy(
-                src_ref=outb.at[0], dst_ref=inb.at[2 * source + j], send_sem=send_sem.at[k, j],
-                recv_sem=recv_sem.at[k, j], device_id={"wide": source}, device_id_type=MESH,
-            ).wait_recv()
+            slot(k, c, j, source, source).wait_recv()
             use(inb[2 * source + j], code_of(info_ref, source, j))
 
-    take((0, 0, 1))
-
-    def arrive(i, carry):
-        chip = i // 2
-        dz = sum(jnp.where(chip == n, z, 0) for n, (z, _) in enumerate(CHIPS))
-        dx = sum(jnp.where(chip == n, x, 0) for n, (_, x) in enumerate(CHIPS))
-        take((dz, dx, i % 2))
-        return carry
-
-    lax.fori_loop(0, 2 * len(CHIPS), arrive, 0)
+    take(0, 1, pair)
+    keep.wait()
+    each(1, 1 + OUT_AHEAD, outward)
+    each(0, 1 + ON_AHEAD, onward)
+    across(0)
+
+    def arrive(k):
+        pl.when(k + BLOCKS_AHEAD <= 15)(lambda: send_block(k + BLOCKS_AHEAD))
+        pl.when(k + TILES_AHEAD <= 15)(lambda: send_tiles(k + TILES_AHEAD))
+        pl.when(k + OUT_AHEAD <= 15)(lambda: outward(k + OUT_AHEAD))
+        dz, dx = step_of(k)
+        for c in range(2):
+            take(k, c, shifted(me, (dz, dx, c), -1))
+        pl.when(k + ON_AHEAD <= 15)(lambda: onward(k + ON_AHEAD))
+        across(k)
+
+    each(1, 16, arrive)
 
     for b in range(NBAT):
         for f in range(FIELDS):
@@ -141,13 +238,32 @@
         swaps.append(copy)
     for copy in sent:
         copy.wait_send()
+    for j in range(2):
+        slot(0, 1, j, pair, me).wait_send()
+
+    def drain(k):
+        plane(k, pair, me).wait_send()
+        for c in range(2):
+            for j in range(2):
+                slot(k, c, j, pair, me).wait_send()
+
+    def finish(k):
+        home = home_of(k)
+        for side, way in enumerate((1, -1)):
+            spread(block, k, home, side, way).wait_send()
+        passed(k, home, row, 1).wait_send()
+        paired(k, home).wait_send()
+        paired(k, shifted(home, (0, 0, 1))).wait_recv()
+
+    each(1, 16, drain)
+    each(0, 16, finish)
     for step, copy in enumerate(swaps):
         copy.wait()
         total = total + parts[step]
     dens_ref[...] = total
 
 
-def dispatch(sel, meta, tiles, ao):
+def dispatch(sel, meta, tiles, ao, occ):
     vmem, smem = pl.BlockSpec(memory_space=pltpu.VMEM), pl.BlockSpec(memory_space=pltpu.SMEM)
     dma = pltpu.SemaphoreType.DMA
     return pl.pallas_call(
@@ -155,35 +271,37 @@
         out_shape=(
             jax.ShapeDtypeStruct((8, PTS), jnp.float32),
             jax.ShapeDtypeStruct((NWIDE, 8, BLK), jnp.int32),
+            jax.ShapeDtypeStruct((NWIDE * SIDE, NOCC, BLK), jnp.bfloat16),
         ),
-        in_specs=[smem, vmem, vmem, vmem],
-        out_specs=(vmem, vmem),
+        in_specs=[smem, vmem, vmem, vmem, vmem],
+        out_specs=(vmem, vmem, pl.BlockSpec(memory_space=pltpu.HBM)),
         scratch_shapes=[
             pltpu.VMEM((2 * NWIDE, ROWS, BLK), jnp.bfloat16),
             pltpu.VMEM((2 * NWIDE, ROWS, BLK), jnp.bfloat16),
             pltpu.VMEM((NBAT, FIELDS, 8, PTS), jnp.float32),
             pltpu.VMEM((8, PTS), jnp.float32),
             pltpu.VMEM((SIDE - 1, 8, PTS), jnp.float32),
+            pltpu.VMEM((NOCC, BLK), jnp.bfloat16),
             dma((NWIDE, 2)), dma((NWIDE, 2)),
             dma((NWIDE,)), dma((NWIDE,)), dma((SIDE - 1,)), dma((SIDE - 1,)),
+            dma, dma((16,)), dma((16,)), dma((16, 2)), dma((16, 2)), dma((16,)), dma((16,)),
+            dma((16,)), dma((16,)),
         ],
         compiler_params=pltpu.CompilerParams(
-            collective_id=0, has_side_effects=True, vmem_limit_bytes=30 * 2**20
+            collective_id=0, has_side_effects=True, vmem_limit_bytes=56 * 2**20
         ),
         cost_estimate=pl.CostEstimate(
             flops=70_000_000_000, bytes_accessed=10_000_000, transcendentals=0
         ),
-    )(sel, meta, tiles, ao)
+    )(sel, meta, tiles, ao, occ)
 
 
 def respond_kernel(
-    code_ref, count_ref, dens_ref, weight_ref, first_ref, second_ref, ao_ref, occ_hbm, vir_hbm,
-    out_ref, occ, vir, pot, scaled, answer, total, left, head, follow, occ_sem, vir_sem,
+    code_ref, count_ref, dens_ref, weight_ref, first_ref, second_ref, ao_ref, occ_hbm,
+    left_hbm, occ, pot, scaled, answer, total, left, head, follow, occ_sem, left_sem,
 ):
     load_occ = pltpu.make_async_copy(occ_hbm, occ, occ_sem)
-    load_vir = pltpu.make_async_copy(vir_hbm, vir, vir_sem)
     load_occ.start()
-    load_vir.start()
 
     lane = lax.broadcasted_iota(jnp.int32, (1, PTS), 1)
     for b in range(NBAT):
@@ -242,66 +360,231 @@
             return follow[r]
 
         lax.while_loop(lambda r: r >= 0, add, head[c])
-        for f in range(FIELDS):
-            left[pl.ds(f * NOCC, NOCC), pl.ds(pl.multiple_of(c * BLK, BLK), BLK)] = total[
-                :, f * BLK : (f + 1) * BLK
-            ].astype(jnp.bfloat16)
+        slot = c % 2
+
+        @pl.when(c >= 2)
+        def _():
+            pltpu.make_async_copy(left.at[slot], left_hbm.at[c], left_sem.at[slot]).wait()
+
+        for half in range(2):
+            for f in range(FIELDS):
+                left[slot, pl.ds(half * HALF + f * 256, 256), :] = total[
+                    half * 256 : (half + 1) * 256, f * BLK : (f + 1) * BLK
+                ].astype(jnp.bfloat16)
+        pltpu.make_async_copy(left.at[slot], left_hbm.at[c], left_sem.at[slot]).start()
         return carry
 
     lax.fori_loop(0, 32, column_sum, 0)
-    load_vir.wait()
-
-    def project(i, carry):
-        q, f = i // FIELDS, i % FIELDS
-        rows = pl.ds(pl.multiple_of(f * NOCC, NOCC), NOCC)
-        out_ref[q, rows, :] = jnp.dot(
-            left[rows, :], vir[:, pl.ds(pl.multiple_of(q * 256, 256), 256)],
-            preferred_element_type=jnp.float32,
-        ).astype(jnp.bfloat16)
-        return carry
-
-    lax.fori_loop(0, SIDE * FIELDS, project, 0)
-
-
-def respond(codes, counts, dens, weights, first, second, ao, occ, vir):
+    for slot in range(2):
+        pltpu.make_async_copy(left.at[slot], left_hbm.at[slot], left_sem.at[slot]).wait()
+
+
+def respond(codes, counts, dens, weights, first, second, ao, occ):
     vmem, smem = pl.BlockSpec(memory_space=pltpu.VMEM), pl.BlockSpec(memory_space=pltpu.SMEM)
-    hbm = pl.BlockSpec(memory_space=pl.ANY)
+    hbm = pl.BlockSpec(memory_space=pltpu.HBM)
     return pl.pallas_call(
         respond_kernel,
-        out_shape=jax.ShapeDtypeStruct((SIDE, FIELDS * NOCC, 256), jnp.bfloat16),
-        in_specs=[smem, smem, vmem, vmem, vmem, vmem, vmem, hbm, hbm],
-        out_specs=vmem,
+        out_shape=jax.ShapeDtypeStruct((32, 2 * HALF, BLK), jnp.bfloat16),
+        in_specs=[smem, smem, vmem, vmem, vmem, vmem, vmem, hbm],
+        out_specs=hbm,
         scratch_shapes=[
             pltpu.VMEM((128, NOCC, BLK), jnp.bfloat16),
-            pltpu.VMEM((4096, NVIR), jnp.bfloat16),
             pltpu.VMEM((8, PTS), jnp.float32),
             pltpu.VMEM((KB * BLK, PTS), jnp.bfloat16),
             pltpu.VMEM((50, BLK, ROWS), jnp.bfloat16),
             pltpu.VMEM((NOCC, ROWS), jnp.float32),
-            pltpu.VMEM((FIELDS * NOCC, 4096), jnp.bfloat16),
+            pltpu.VMEM((2, 2 * HALF, BLK), jnp.bfloat16),
             pltpu.SMEM((32,), jnp.int32),
             pltpu.SMEM((64,), jnp.int32),
             pltpu.SemaphoreType.DMA,
-            pltpu.SemaphoreType.DMA,
+            pltpu.SemaphoreType.DMA((2,)),
         ],
         compiler_params=pltpu.CompilerParams(vmem_limit_bytes=62 * 2**20),
         cost_estimate=pl.CostEstimate(
             flops=30_000_000_000, bytes_accessed=30_000_000, transcendentals=0
         ),
-    )(codes, counts, dens, weights, first, second, ao, occ, vir)
-
-
-def turn_kernel(occ_ref, out_ref):
+    )(codes, counts, dens, weights, first, second, ao, occ)
+
+
+def reduce_kernel(
+    left_hbm, vir_hbm, out_ref, left, vir, give, got, mid, y_one, x_one, y_sum, x_sum, x_two, y_two,
+    left_sem, vir_sem, give_send, give_recv, y_one_send, y_one_recv, x_one_send, x_one_recv,
+    x_two_send, x_two_recv, y_two_send, y_two_recv,
+):
+    me = lax.axis_index("wide")
     row = lax.axis_index("narrow")
-    out_ref[...] = occ_ref[pl.ds(pl.multiple_of(row * BLK, BLK), BLK), :].T
-
-
-def turned(occ):
-    vmem = pl.BlockSpec(memory_space=pltpu.VMEM)
+    core, chip = me % 2, me // 2
+    pair = shifted(me, (0, 0, 1))
+    peers = [shifted(me, (z, x, 0)) for z, x in CHIPS]
+    barrier = pltpu.get_barrier_semaphore()
+    for peer in [pair, *peers]:
+        pl.semaphore_signal(barrier, inc=1, device_id={"wide": peer}, device_id_type=MESH)
+    for step in range(1, SIDE):
+        pl.semaphore_signal(
+            barrier, inc=1, device_id={"narrow": (row + step) % SIDE}, device_id_type=MESH
+        )
+
+    def load(half, c):
+        rows = pl.ds(pl.multiple_of(half * HALF, HALF), HALF)
+        return pltpu.make_async_copy(
+            left_hbm.at[c, rows],
+            left.at[half, :, pl.ds(pl.multiple_of(c * BLK, BLK), BLK)],
+            left_sem.at[half, c],
+        )
+
+    def load_vir(q):
+        return pltpu.make_async_copy(
+            vir_hbm.at[:, pl.ds(pl.multiple_of(q * 256, 256), 256)], vir.at[q], vir_sem.at[q]
+        )
+
+    def each(last, step):
+        def run(k, carry):
+            step(k)
+            return carry
+
+        lax.fori_loop(0, last, run, 0)
+
+    load_vir(0).start()
+    each(32, lambda c: load(1 - core, c).start())
+    for q in range(1, SIDE):
+        load_vir(q).start()
+    each(32, lambda c: load(core, c).start())
+    pl.semaphore_wait(barrier, 1 + len(peers) + SIDE - 1)
+
+    def to(axis, peer, src, dst, ssem, rsem):
+        return pltpu.make_async_remote_copy(
+            src_ref=src, dst_ref=dst, send_sem=ssem, recv_sem=rsem, device_id={axis: peer},
+            device_id_type=MESH,
+        )
+
+    def product(half, q):
+        return jnp.dot(left[half], vir[q], preferred_element_type=jnp.float32).reshape(
+            FIELDS, 256, 256
+        )
+
+    def hand(q):
+        return to("wide", pair, give.at[q], got.at[q], give_send.at[q], give_recv.at[q])
+
+    def other_half(q):
+        load_vir(q).wait()
+        give[q] = product(1 - core, q).astype(jnp.bfloat16)
+        hand(q).start()
+
+    each(32, lambda c: load(1 - core, c).wait())
+    each(SIDE, other_half)
+    each(32, lambda c: load(core, c).wait())
+
+    def down(q, y):
+        return to(
+            "narrow", q, mid.at[q, :, :, pl.ds(0, BLK)], y_one.at[y], y_one_send.at[q],
+            y_one_recv.at[y],
+        )
+
+    def over(q, k, peer):
+        rows = pl.ds(pl.multiple_of((peer // 2) * 16, 16), 16)
+        return to(
+            "wide", peer, mid.at[q, :, rows, pl.ds(BLK, BLK)], x_one.at[k, q],
+            x_one_send.at[k, q], x_one_recv.at[k, q],
+        )
+
+    def own_half(q):
+        own = product(core, q)
+        hand(q).wait_recv()
+        mid[q] = (own + got[q].astype(jnp.float32)).astype(jnp.bfloat16)
+        pl.when(q != row)(lambda: down(q, row).start())
+        for k, peer in enumerate(peers):
+            over(q, k, peer).start()
+
+    each(SIDE, own_half)
+    here = pl.ds(pl.multiple_of(chip * 16, 16), 16)
+
+    total = mid[row, :, :, pl.ds(0, BLK)].astype(jnp.float32)
+    for step in range(1, SIDE):
+        y = (row + step) % SIDE
+        down(y, y).wait_recv()
+        total = total + y_one[y].astype(jnp.float32)
+    y_sum[...] = total.astype(jnp.bfloat16)
+
+    def scatter(k, peer):
+        rows = pl.ds(pl.multiple_of((peer // 2) * 16, 16), 16)
+        return to("wide", peer, y_sum.at[:, rows], x_two.at[k], x_two_send.at[k], x_two_recv.at[k])
+
+    for k, peer in enumerate(peers):
+        scatter(k, peer).start()
+
+    total = mid[:, :, here, pl.ds(BLK, BLK)].astype(jnp.float32)
+    for k, peer in enumerate(peers):
+        for q in range(SIDE):
+            over(q, k, peer).wait_recv()
+        total = total + x_one[k].astype(jnp.float32)
+    x_sum[...] = total.astype(jnp.bfloat16)
+
+    def give_row(step):
+        y = (row + step) % SIDE
+        return to(
+            "narrow", y, x_sum.at[y], y_two.at[step - 1], y_two_send.at[step - 1],
+            y_two_recv.at[step - 1],
+        )
+
+    for step in range(1, SIDE):
+        give_row(step).start()
+
+    total = y_sum[:, here].astype(jnp.float32)
+    for k, peer in enumerate(peers):
+        scatter(k, peer).wait_recv()
+        total = total + x_two[k].astype(jnp.float32)
+    out_ref[:, :, pl.ds(0, BLK)] = total
+    total = x_sum[row].astype(jnp.float32)
+    for step in range(1, SIDE):
+        give_row(step).wait_recv()
+        total = total + y_two[step - 1].astype(jnp.float32)
+    out_ref[:, :, pl.ds(BLK, BLK)] = total
+
+    def sent(q):
+        hand(q).wait_send()
+        pl.when(q != row)(lambda: down(q, row).wait_send())
+        for k, peer in enumerate(peers):
+            over(q, k, peer).wait_send()
+
+    each(SIDE, sent)
+    for k, peer in enumerate(peers):
+        scatter(k, peer).wait_send()
+    for step in range(1, SIDE):
+        give_row(step).wait_send()
+
+
+def reduced(left, vir):
+    hbm = pl.BlockSpec(memory_space=pltpu.HBM)
+    dma, bf16 = pltpu.SemaphoreType.DMA, jnp.bfloat16
+    chips = len(CHIPS)
     return pl.pallas_call(
-        turn_kernel, out_shape=jax.ShapeDtypeStruct((NOCC, BLK), occ.dtype), in_specs=[vmem],
-        out_specs=vmem,
-    )(occ)
+        reduce_kernel,
+        out_shape=jax.ShapeDtypeStruct((FIELDS, 16, 256), jnp.float32),
+        in_specs=[hbm, hbm],
+        out_specs=pl.BlockSpec(memory_space=pltpu.VMEM),
+        scratch_shapes=[
+            pltpu.VMEM((2, HALF, 4096), bf16),
+            pltpu.VMEM((SIDE, 4096, 256), bf16),
+            pltpu.VMEM((SIDE, FIELDS, 256, 256), bf16),
+            pltpu.VMEM((SIDE, FIELDS, 256, 256), bf16),
+            pltpu.VMEM((SIDE, FIELDS, 256, 256), bf16),
+            pltpu.VMEM((SIDE, FIELDS, 256, BLK), bf16),
+            pltpu.VMEM((chips, SIDE, FIELDS, 16, BLK), bf16),
+            pltpu.VMEM((FIELDS, 256, BLK), bf16),
+            pltpu.VMEM((SIDE, FIELDS, 16, BLK), bf16),
+            pltpu.VMEM((chips, FIELDS, 16, BLK), bf16),
+            pltpu.VMEM((SIDE - 1, FIELDS, 16, BLK), bf16),
+            dma((2, 32)), dma((SIDE,)), dma((SIDE,)), dma((SIDE,)), dma((SIDE,)), dma((SIDE,)),
+            dma((chips, SIDE)), dma((chips, SIDE)), dma((chips,)), dma((chips,)),
+            dma((SIDE - 1,)), dma((SIDE - 1,)),
+        ],
+        compiler_params=pltpu.CompilerParams(
+            collective_id=1, has_side_effects=True, vmem_limit_bytes=50 * 2**20
+        ),
+        cost_estimate=pl.CostEstimate(
+            flops=30_000_000_000, bytes_accessed=30_000_000, transcendentals=0
+        ),
+    )(left, vir)
 
 
 def body(
@@ -319,9 +602,6 @@
     vir_coef,
 ):
     tile_count = dens_tiles.shape[0]
-    block = turned(occ_coef)
-    occ_all = lax.all_gather(block[None], ("wide", "narrow"), axis=0, tiled=True)
-
     targets = tile_dest.reshape(-1)
     routes = jnp.arange(targets.shape[0])
     earlier = (targets[:, None] == targets[None, :]) & (routes[:, None] > routes[None, :])
@@ -340,19 +620,14 @@
     )
 
     ao = ao_values.reshape(NBAT * KB, BLK, PTS)
-    dens, info = dispatch(sel, meta, dens_tiles.reshape(tile_count, ROWS, BLK), ao)
-    partial = respond(
+    dens, info, occ_all = dispatch(
+        sel, meta, dens_tiles.reshape(tile_count, ROWS, BLK), ao, occ_coef
+    )
+    left = respond(
         info[:, 0, :2].reshape(-1), point_count, dens, weights, kernel_first, kernel_second, ao,
-        occ_all, vir_coef,
+        occ_all,
     )
-
-    parts = lax.all_to_all(
-        partial.reshape(SIDE, FIELDS, NOCC, 256), "narrow", 0, 0, tiled=True
-    )
-    by_columns = jnp.sum(parts.astype(jnp.float32), axis=0).astype(jnp.bfloat16)
-    split = jnp.moveaxis(by_columns.reshape(FIELDS, NWIDE, NOCC // NWIDE, 256), 1, 0)
-    owned = lax.all_to_all(split, "wide", 0, 0, tiled=True)
-    return jnp.sum(owned.astype(jnp.float32), axis=0)
+    return reduced(left, vir_coef)
 
 
 def solution(mesh):

time: 270 us -> 209 us (0.77)
  blocking collectives: 62.3 us -> 0 us
  Pallas kernels: 144 us -> 199 us
  waiting for transfers between devices: 35.6 us -> 0 us
  between operations: 13.5 us -> 0.08 us
  local copies, waits for them, and re-layouts: 7.8 us -> 4.82 us
    all_to_all x2 -> x0, blocking collectives: 62.3 us -> none  [the longest x1 43.3 us: body(): lax.all_to_all(partial.reshape(SIDE, FIELDS, NOCC, 256), 'narrow', 0, 0,...]
    all_gather x1 -> x0, waiting for transfers between devices: 35.6 us -> none  [body(): lax.all_gather(block[None], ('wide', 'narrow'), axis=0, tiled=True)]
    pallas_call x1, Pallas kernels: 100 us -> 129 us  [dispatch(): pl.pallas_call(dispatch_kernel, out_shape=(jax.ShapeDtypeStruct((8, PTS),...]
    pallas_call x2, Pallas kernels: 44.3 us -> 69.9 us  [the longest x1 42.5 us: reduced(): pl.pallas_call(reduce_kernel, out_shape=jax.ShapeDtypeStruct((FIELDS, 16,...]
    unnamed x7 -> x2, local copies, waits for them, and re-layouts: 4.7 us -> 1.38 us
  transfers between devices with their start and end apart: 1 -> 0, of which waited for: 1 -> 0; matrix products, arithmetic and copies ran while one was open for 2% -> 0% of each run, Pallas kernels for 37% -> 0%
where the time goes in v2:
time: 209 us; the launch traced here: 207 us
  Pallas kernels  199 us (95%)
  local copies, waits for them, and re-layouts  4.82 us (2%)
  other arithmetic  3.51 us (2%)
    pallas_call x1, Pallas kernels, dispatch(): pl.pallas_call(dispatch_kernel, out_shape=(jax.ShapeDtypeStruct((8, PTS),...  129 us
    pallas_call x1, Pallas kernels, reduced(): pl.pallas_call(reduce_kernel, out_shape=jax.ShapeDtypeStruct((FIELDS, 16,...  42.5 us
    pallas_call x1, Pallas kernels, respond(): pl.pallas_call(respond_kernel, out_shape=jax.ShapeDtypeStruct((32, 2 * HA...  27.4 us

profile of v2, /device:TPU:0, one launch (start us, length us, event | category | flops | bytes accessed | tf_op | source)
XLA Modules:
  0.0 207.0 jit_solution(9002274862580326398)
XLA Ops:
  0.0 0.7 broadcast_multiply_fusion.2
  0.7 0.7 broadcast_multiply_fusion.1
  1.3 0.7 sign_compare_fusion
  2.0 0.1 copy.24
  2.1 0.1 ne.92
  2.2 0.7 broadcast_divide_fusion
  2.9 0.1 copy.26
  3.0 0.1 div.29
  3.1 0.1 broadcast_in_dim.40
  3.1 0.1 mul.94
  3.2 0.1 broadcast_in_dim.39
  3.3 0.1 mul.91
  3.4 0.1 copy.25
  3.5 0.1 rem.42
  3.6 0.1 copy.27
  3.7 0.1 mul.88
  3.8 0.8 copy.23
  4.5 0.1 reshape.134
  4.6 0.2 convert_reduce_fusion
  4.8 0.6 select_reduce_fusion
  5.4 0.1 reshape.135
  5.5 0.7 broadcast_in_dim.43.meta_ref
  6.2 128.7 %shard_map.118 = (f32[8,1280]{1,0:T(8,128)}, s32[32,8,128]{2,1,0:T(8,128)}, bf16[128,512,128]{2,1,0:T(8,128)(2,1)}) custom-call(s32[64]{0:T(128)} %get-tuple-element.12.sel_ref, s32[32,8,128]{2,1,0:T(8,128)} %broadcast_in_dim.43.meta_ref, bf16[16,384,128]{2,1,0:T(8,128)(2,1)} %bitcast.6, bf16[10,128,1280]{2,1,0:T(8,128)(2,1)} %bitcast.4, ...), custom_call_target="tpu_custom_call" | custom-call | flops 70000001024 | bytes 10000000 | tf_op jit(solution)/shard_map/pallas_call | solution.py:269
  135.0 0.9 slice_reduce_fusion
  135.9 0.6 reshape_squeeze.3.code_ref
  136.5 27.4 %shard_map.119.left_hbm = bf16[32,1536,128]{2,1,0:T(8,128)(2,1)} custom-call(s32[64]{0:T(128)} %reshape_squeeze.3.code_ref, s32[2]{0:T(128)} %count_ref.1, f32[8,1280]{1,0:T(8,128)} %get-tuple-element.9.dens_ref, f32[2,1280]{1,0:T(2,128)} %weight_ref.1, f32[2,1280]{1,0:T(2,128)} %first_ref.1, f32[2,1280]{1,0:T(2,128)} %second_ref.1, ...), custom_call_target="tpu_custom_call" | custom-call | flops 30000001024 | bytes 30000000 | tf_op jit(solution)/shard_map/pallas_call | solution.py:385
  163.9 42.5 %shard_map.120 = f32[3,16,256]{2,1,0:T(8,128)S(1)} custom-call(bf16[32,1536,128]{2,1,0:T(8,128)(2,1)} %shard_map.119.left_hbm, bf16[4096,1024]{1,0:T(8,128)(2,1)} %vir_hbm.1), custom_call_target="tpu_custom_call" | custom-call | flops 30000001024 | bytes 30000000 | tf_op jit(solution)/shard_map/pallas_call | solution.py:560
  206.4 0.6 copy.29
  (3 shorter events, 0.0 us)

commit v3 on v2

--- a/solution.py
+++ b/solution.py
@@ -18,7 +18,7 @@
 HALF = FIELDS * NOCC // 2
 MESH = pl.DeviceIdType.MESH
 CHIPS = [(2, 2), (1, 1), (3, 3), (1, 3), (3, 1), (1, 2), (3, 2), (2, 1), (2, 3), (0, 2), (2, 0), (0, 1), (0, 3), (1, 0), (3, 0)]
-BLOCKS_AHEAD, OUT_AHEAD, TILES_AHEAD, ON_AHEAD = 11, 8, 6, 4
+OUT_AHEAD, TILES_AHEAD, ON_AHEAD = 8, 6, 4
 OFFSETS = [(z, x, c) for z, x in CHIPS for c in range(2)] + [(0, 0, 1)]
 
 
@@ -35,8 +35,8 @@
 
 
 def dispatch_kernel(
-    sel_ref, meta_ref, tiles_ref, ao_ref, occ_ref, dens_ref, info_ref, all_ref,
-    outb, inb, acc, mine, parts, block,
+    sel_ref, meta_ref, tiles_ref, ao_ref, occ_ref, dens_ref, codes_ref, all_ref,
+    info_ref, outb, inb, acc, mine, parts, block,
     send_sem, recv_sem, meta_send, meta_recv, part_send, part_recv,
     own_sem, plane_send, plane_recv, side_send, side_recv, pass_send, pass_recv, pair_send, pair_recv,
 ):
@@ -84,8 +84,14 @@
         dx = sum(jnp.where(k == n + 1, x, 0) for n, (_, x) in enumerate(CHIPS))
         return dz, dx
 
+    core = me % 2
+
+    def turn(k):
+        d, e = k % 4, k // 4
+        return e + core * (d - e), d + core * (e - d)
+
     def home_of(k):
-        return shifted(me, (*step_of(k), 0), -1)
+        return shifted(me, (*turn(k), 0), -1)
 
     def slot(k, c, j, peer, source):
         return pltpu.make_async_remote_copy(
@@ -103,14 +109,14 @@
     def place(home, y):
         return all_ref.at[home * SIDE + (y + 2 * SIDE) % SIDE]
 
-    def plane(k, peer, home):
+    def plane(k, peer, home, src=block):
         return pltpu.make_async_remote_copy(
-            src_ref=block, dst_ref=place(home, row), send_sem=plane_send.at[k],
+            src_ref=src, dst_ref=place(home, row), send_sem=plane_send.at[k],
             recv_sem=plane_recv.at[k], device_id={"wide": peer}, device_id_type=MESH,
         )
 
     def send_block(k):
-        plane(k, shifted(me, (*step_of(k), 0)), me).start()
+        plane(k, shifted(me, (*turn(k), 0)), me).start()
 
     def spread(src, k, home, side, way):
         return pltpu.make_async_remote_copy(
@@ -138,6 +144,13 @@
         plane(k, home, home).wait_recv()
         for side, way in enumerate((1, -1)):
             spread(place(home, row), k, home, side, way).start()
+
+    def forward(k):
+        home = home_of(k)
+        for e in range(1, SIDE):
+            plane(
+                4 * e + k, shifted(me, (*turn(4 * e), 0)), home, place(home, row)
+            ).start()
 
     def onward(k):
         home = home_of(k)
@@ -167,10 +180,18 @@
     for side, way in enumerate((1, -1)):
         spread(block, 0, me, side, way).start()
     pair = shifted(me, (0, 0, 1))
+    for k in (1, 2, 3, 4, 8, 12):
+        send_block(k)
     for j in range(2):
         slot(0, 1, j, pair, me).start()
-    each(1, 1 + BLOCKS_AHEAD, send_block)
-    each(1, 1 + TILES_AHEAD, send_tiles)
+    send_tiles(1)
+
+    def relay(k):
+        outward(k)
+        forward(k)
+
+    each(1, SIDE, relay)
+    each(2, 1 + TILES_AHEAD, send_tiles)
 
     def use(tile, code):
         first, second = code % 16, (code // 16) % 16
@@ -190,7 +211,9 @@
         return ref[source, 0:1, j : j + 1][0, 0]
 
     for j in range(2):
-        use(outb[2 * me + j], code_of(meta_ref, me, j))
+        code = code_of(meta_ref, me, j)
+        codes_ref[2 * me + j] = code
+        use(outb[2 * me + j], code)
 
     for offset in OFFSETS:
         peer, k = shifted(me, offset), number(offset)
@@ -202,16 +225,17 @@
     def take(k, c, source):
         for j in range(2):
             slot(k, c, j, source, source).wait_recv()
-            use(inb[2 * source + j], code_of(info_ref, source, j))
+            code = code_of(info_ref, source, j)
+            codes_ref[2 * source + j] = code
+            use(inb[2 * source + j], code)
 
     take(0, 1, pair)
     keep.wait()
-    each(1, 1 + OUT_AHEAD, outward)
+    each(SIDE, 1 + OUT_AHEAD, outward)
     each(0, 1 + ON_AHEAD, onward)
     across(0)
 
     def arrive(k):
-        pl.when(k + BLOCKS_AHEAD <= 15)(lambda: send_block(k + BLOCKS_AHEAD))
         pl.when(k + TILES_AHEAD <= 15)(lambda: send_tiles(k + TILES_AHEAD))
         pl.when(k + OUT_AHEAD <= 15)(lambda: outward(k + OUT_AHEAD))
         dz, dx = step_of(k)
@@ -253,7 +277,8 @@
             spread(block, k, home, side, way).wait_send()
         passed(k, home, row, 1).wait_send()
         paired(k, home).wait_send()
-        paired(k, shifted(home, (0, 0, 1))).wait_recv()
+        dz, dx = turn(k)
+        paired(k, shifted(me, (dx, dz, 1), -1)).wait_recv()
 
     each(1, 16, drain)
     each(0, 16, finish)
@@ -270,12 +295,13 @@
         dispatch_kernel,
         out_shape=(
             jax.ShapeDtypeStruct((8, PTS), jnp.float32),
-            jax.ShapeDtypeStruct((NWIDE, 8, BLK), jnp.int32),
+            jax.ShapeDtypeStruct((2 * NWIDE,), jnp.int32),
             jax.ShapeDtypeStruct((NWIDE * SIDE, NOCC, BLK), jnp.bfloat16),
         ),
         in_specs=[smem, vmem, vmem, vmem, vmem],
-        out_specs=(vmem, vmem, pl.BlockSpec(memory_space=pltpu.HBM)),
+        out_specs=(vmem, smem, pl.BlockSpec(memory_space=pltpu.HBM)),
         scratch_shapes=[
+            pltpu.VMEM((NWIDE, 8, BLK), jnp.int32),
             pltpu.VMEM((2 * NWIDE, ROWS, BLK), jnp.bfloat16),
             pltpu.VMEM((2 * NWIDE, ROWS, BLK), jnp.bfloat16),
             pltpu.VMEM((NBAT, FIELDS, 8, PTS), jnp.float32),
@@ -330,6 +356,8 @@
 
     def clear(c, carry):
         head[c] = -1
+        follow[2 * c] = -1
+        follow[2 * c + 1] = -1
         return carry
 
     lax.fori_loop(0, 32, clear, 0)
@@ -349,17 +377,40 @@
     load_occ.wait()
 
     def column_sum(c, carry):
-        total[...] = jnp.zeros_like(total)
+        def term(r):
+            code = code_ref[r]
+            return occ[(r // 2) * 4 + (code // 65536) % 4], answer[(code // 512) % 64]
+
+        def two(r):
+            nxt = follow[r]
+            other = jnp.where(nxt >= 0, nxt, r)
+            (left_a, right_a), (left_b, right_b) = term(r), term(other)
+            right_b = jnp.where(nxt >= 0, right_b, jnp.zeros_like(right_b))
+            return jnp.dot(
+                jnp.concatenate([left_a, left_b], axis=1),
+                jnp.concatenate([right_a, right_b], axis=0), preferred_element_type=jnp.float32,
+            )
+
+        def after(r):
+            nxt = follow[jnp.maximum(r, 0)]
+            last = jnp.logical_or(r < 0, nxt < 0)
+            return jnp.where(last, -1, follow[jnp.maximum(nxt, 0)])
 
         def add(r):
-            code = code_ref[r]
-            block = (r // 2) * 4 + (code // 65536) % 4
-            total[...] += jnp.dot(
-                occ[block], answer[(code // 512) % 64], preferred_element_type=jnp.float32
-            )
-            return follow[r]
-
-        lax.while_loop(lambda r: r >= 0, add, head[c])
+            total[...] += two(r)
+            return after(r)
+
+        first = head[c]
+
+        @pl.when(first < 0)
+        def _():
+            total[...] = jnp.zeros_like(total)
+
+        @pl.when(first >= 0)
+        def _():
+            total[...] = two(first)
+
+        lax.while_loop(lambda r: r >= 0, add, after(first))
         slot = c % 2
 
         @pl.when(c >= 2)
@@ -614,17 +665,17 @@
     )
     chosen = position[None, :] == jnp.arange(2 * NWIDE)[:, None]
     sel = jnp.sum(jnp.where(chosen, routes[None, :] // 2, 0), axis=1)
-    codes = jnp.sum(jnp.where(chosen, code[None, :], 0), axis=1)
+    sent = jnp.sum(jnp.where(chosen, code[None, :], 0), axis=1)
     meta = jnp.broadcast_to(
-        jnp.pad(codes.reshape(NWIDE, 1, 2), ((0, 0), (0, 0), (0, BLK - 2))), (NWIDE, 8, BLK)
+        jnp.pad(sent.reshape(NWIDE, 1, 2), ((0, 0), (0, 0), (0, BLK - 2))), (NWIDE, 8, BLK)
     )
 
     ao = ao_values.reshape(NBAT * KB, BLK, PTS)
-    dens, info, occ_all = dispatch(
+    dens, codes, occ_all = dispatch(
         sel, meta, dens_tiles.reshape(tile_count, ROWS, BLK), ao, occ_coef
     )
     left = respond(
-        info[:, 0, :2].reshape(-1), point_count, dens, weights, kernel_first, kernel_second, ao,
+        codes, point_count, dens, weights, kernel_first, kernel_second, ao,
         occ_all,
     )
     return reduced(left, vir_coef)

time: 209 us -> 189 us (0.904)
  Pallas kernels: 199 us -> 181 us
    pallas_call x1, Pallas kernels: 129 us -> 117 us  [dispatch(): pl.pallas_call(dispatch_kernel, out_shape=(jax.ShapeDtypeStruct((8, PTS),...]
    pallas_call x1, Pallas kernels: 42.5 us -> 37.7 us  [reduced(): pl.pallas_call(reduce_kernel, out_shape=jax.ShapeDtypeStruct((FIELDS, 16,...]
where the time goes in v3:
time: 189 us; the launch traced here: 188 us
  Pallas kernels  181 us (96%)
  other arithmetic  3.51 us (2%)
  local copies, waits for them, and re-layouts  3.25 us (2%)
    pallas_call x1, Pallas kernels, dispatch(): pl.pallas_call(dispatch_kernel, out_shape=(jax.ShapeDtypeStruct((8, PTS),...  117 us
    pallas_call x1, Pallas kernels, reduced(): pl.pallas_call(reduce_kernel, out_shape=jax.ShapeDtypeStruct((FIELDS, 16,...  37.7 us
    pallas_call x1, Pallas kernels, respond(): pl.pallas_call(respond_kernel, out_shape=jax.ShapeDtypeStruct((32, 2 * HA...  26.6 us

profile of v3, /device:TPU:0, one launch (start us, length us, event | category | flops | bytes accessed | tf_op | source)
XLA Modules:
  0.0 187.7 jit_solution(18182596293679974861)
XLA Ops:
  0.0 0.7 broadcast_multiply_fusion.2
  0.7 0.7 broadcast_multiply_fusion.1
  1.3 0.7 sign_compare_fusion
  2.0 0.1 copy.24
  2.1 0.1 ne.92
  2.2 0.7 broadcast_divide_fusion
  2.9 0.1 copy.26
  3.0 0.1 div.29
  3.1 0.1 broadcast_in_dim.40
  3.1 0.1 mul.94
  3.2 0.1 broadcast_in_dim.39
  3.3 0.1 mul.91
  3.4 0.1 copy.25
  3.5 0.1 rem.42
  3.6 0.1 copy.27
  3.7 0.1 mul.88
  3.8 0.8 copy.23
  4.5 0.1 reshape.134
  4.6 0.2 convert_reduce_fusion
  4.8 0.6 select_reduce_fusion
  5.4 0.1 reshape.135
  5.5 0.7 broadcast_in_dim.43.meta_ref
  6.2 116.6 %shard_map.118 = (f32[8,1280]{1,0:T(8,128)}, s32[64]{0:T(128)}, bf16[128,512,128]{2,1,0:T(8,128)(2,1)}) custom-call(s32[64]{0:T(128)} %get-tuple-element.12.sel_ref, s32[32,8,128]{2,1,0:T(8,128)} %broadcast_in_dim.43.meta_ref, bf16[16,384,128]{2,1,0:T(8,128)(2,1)} %bitcast.6, bf16[10,128,1280]{2,1,0:T(8,128)(2,1)} %bitcast.4, bf16[512,512]{1,0:T(8,128)(2,1)} %occ_ref.1), custom_call_target="tpu_custom_call" | custom-call | flops 70000001024 | bytes 10000000 | tf_op jit(solution)/shard_map/pallas_call | solution.py:294
  122.8 26.6 %shard_map.119.left_hbm = bf16[32,1536,128]{2,1,0:T(8,128)(2,1)} custom-call(s32[64]{0:T(128)} %get-tuple-element.8.code_ref, s32[2]{0:T(128)} %count_ref.1, f32[8,1280]{1,0:T(8,128)} %get-tuple-element.9.dens_ref, f32[2,1280]{1,0:T(2,128)} %weight_ref.1, f32[2,1280]{1,0:T(2,128)} %first_ref.1, f32[2,1280]{1,0:T(2,128)} %second_ref.1, ...), custom_call_target="tpu_custom_call" | custom-call | flops 30000001024 | bytes 30000000 | tf_op jit(solution)/shard_map/pallas_call | solution.py:436
  149.4 37.7 %shard_map.120 = f32[3,16,256]{2,1,0:T(8,128)S(1)} custom-call(bf16[32,1536,128]{2,1,0:T(8,128)(2,1)} %shard_map.119.left_hbm, bf16[4096,1024]{1,0:T(8,128)(2,1)} %vir_hbm.1), custom_call_target="tpu_custom_call" | custom-call | flops 30000001024 | bytes 30000000 | tf_op jit(solution)/shard_map/pallas_call | solution.py:611
  187.1 0.6 copy.29
  (3 shorter events, 0.0 us)

commit v4 on v3

--- a/solution.py
+++ b/solution.py
@@ -14,6 +14,7 @@
 PTS = 1280
 SIDE = 4
 NWIDE = 32
+TILES = 16
 ROWS = FIELDS * BLK
 HALF = FIELDS * NOCC // 2
 MESH = pl.DeviceIdType.MESH
@@ -30,18 +31,21 @@
     return z * 8 + x * 2 + c
 
 
-def number(offset):
-    return offset[0] * 8 + offset[1] * 2 + offset[2]
-
-
 def dispatch_kernel(
-    sel_ref, meta_ref, tiles_ref, ao_ref, occ_ref, dens_ref, codes_ref, all_ref,
-    info_ref, outb, inb, acc, mine, parts, block,
+    dest_ref, place_ref, rows_ref, cols_ref, tiles_hbm, ao_hbm, occ_hbm, dens_ref, codes_ref, all_ref,
+    tiles_ref, ao_ref, occ_ref, load_sem, meta_ref, info_ref, outb, inb, acc, mine, parts, block,
     send_sem, recv_sem, meta_send, meta_recv, part_send, part_recv,
     own_sem, plane_send, plane_recv, side_send, side_recv, pass_send, pass_recv, pair_send, pair_recv,
 ):
     me = lax.axis_index("wide")
     row = lax.axis_index("narrow")
+    quarter = pl.ds(pl.multiple_of(row * BLK, BLK), BLK)
+    load_occ = pltpu.make_async_copy(occ_hbm.at[quarter], occ_ref, load_sem.at[0])
+    load_tiles = pltpu.make_async_copy(tiles_hbm, tiles_ref, load_sem.at[1])
+    load_ao = pltpu.make_async_copy(ao_hbm, ao_ref, load_sem.at[2])
+    load_occ.start()
+    load_tiles.start()
+    load_ao.start()
     barrier = pltpu.get_barrier_semaphore()
     for offset in OFFSETS:
         pl.semaphore_signal(
@@ -52,32 +56,13 @@
             barrier, inc=1, device_id={"narrow": (row + step) % SIDE}, device_id_type=MESH
         )
 
-    turned = occ_ref[pl.ds(pl.multiple_of(row * BLK, BLK), BLK), :].T
+    load_occ.wait()
+    turned = occ_ref[...].T
     for w in range(NWIDE):
         block[pl.ds((w % 2) * 256 + (w // 2) * 16, 16), :] = turned[w * 16 : (w + 1) * 16]
 
-    def build(i, carry):
-        outb[i] = tiles_ref[sel_ref[i]]
-        return carry
-
-    lax.fori_loop(0, 2 * NWIDE, build, 0)
     acc[...] = jnp.zeros_like(acc)
     pl.semaphore_wait(barrier, len(OFFSETS) + SIDE - 1)
-
-    sent = []
-
-    def send(src, dst, ssem, rsem, peer):
-        copy = pltpu.make_async_remote_copy(
-            src_ref=src, dst_ref=dst, send_sem=ssem, recv_sem=rsem,
-            device_id={"wide": peer}, device_id_type=MESH,
-        )
-        copy.start()
-        sent.append(copy)
-
-    for offset in OFFSETS:
-        peer, k = shifted(me, offset), number(offset)
-        send(meta_ref.at[peer], info_ref.at[me], meta_send.at[k], meta_recv.at[k], peer)
-    info_ref[me] = meta_ref[me]
 
     def step_of(k):
         dz = sum(jnp.where(k == n + 1, z, 0) for n, (z, _) in enumerate(CHIPS))
@@ -100,9 +85,16 @@
             device_id={"wide": peer}, device_id_type=MESH,
         )
 
+    def info(k, peer, source):
+        return pltpu.make_async_remote_copy(
+            src_ref=meta_ref.at[peer], dst_ref=info_ref.at[source], send_sem=meta_send.at[k],
+            recv_sem=meta_recv.at[k], device_id={"wide": peer}, device_id_type=MESH,
+        )
+
     def send_tiles(k):
         dz, dx = step_of(k)
         for c in range(2):
+            info(2 * k + c, shifted(me, (dz, dx, c)), me).start()
             for j in range(2):
                 slot(k, c, j, shifted(me, (dz, dx, c)), me).start()
 
@@ -182,16 +174,54 @@
     pair = shifted(me, (0, 0, 1))
     for k in (1, 2, 3, 4, 8, 12):
         send_block(k)
+    load_tiles.wait()
+    lane = lax.broadcasted_iota(jnp.int32, (8, BLK), 1)
+
+    def route(peer):
+        found = [-1, -1]
+        for r in range(2 * TILES):
+            hit = dest_ref[r % 2, r // 2] == peer
+            found = [
+                jnp.where(jnp.logical_and(hit, found[0] < 0), r, found[0]),
+                jnp.where(jnp.logical_and(hit, found[0] >= 0), r, found[1]),
+            ]
+        codes = []
+        for j in range(2):
+            r = jnp.maximum(found[j], 0)
+            t = r // 2
+            spot = place_ref[r % 2, t]
+            batch, block_pair = spot // 25, spot % 25
+            code = (
+                (batch * KB + block_pair // KB) + 16 * (batch * KB + block_pair % KB) + 256 * batch
+                + 512 * spot + 32768 + 65536 * rows_ref[t] + 262144 * cols_ref[t]
+            )
+            codes.append(jnp.where(found[j] >= 0, code, 0))
+            outb[2 * peer + j] = tiles_ref[t]
+        meta_ref[peer] = jnp.where(lane == 0, codes[0], jnp.where(lane == 1, codes[1], 0))
+
+    def route_chip(k):
+        dz, dx = step_of(k)
+        for c in range(2):
+            route(shifted(me, (dz, dx, c)))
+
+    def advance(k):
+        pl.when(k < 15)(lambda: route_chip(k + 1))
+        send_tiles(k)
+
+    route(pair)
+    route(me)
+    route_chip(1)
+    info(1, pair, me).start()
     for j in range(2):
         slot(0, 1, j, pair, me).start()
-    send_tiles(1)
+    advance(1)
 
     def relay(k):
         outward(k)
         forward(k)
 
     each(1, SIDE, relay)
-    each(2, 1 + TILES_AHEAD, send_tiles)
+    each(2, 1 + TILES_AHEAD, advance)
 
     def use(tile, code):
         first, second = code % 16, (code // 16) % 16
@@ -210,19 +240,14 @@
     def code_of(ref, source, j):
         return ref[source, 0:1, j : j + 1][0, 0]
 
+    load_ao.wait()
     for j in range(2):
         code = code_of(meta_ref, me, j)
         codes_ref[2 * me + j] = code
         use(outb[2 * me + j], code)
 
-    for offset in OFFSETS:
-        peer, k = shifted(me, offset), number(offset)
-        pltpu.make_async_remote_copy(
-            src_ref=meta_ref.at[0], dst_ref=info_ref.at[0], send_sem=meta_send.at[k],
-            recv_sem=meta_recv.at[k], device_id={"wide": peer}, device_id_type=MESH,
-        ).wait_recv()
-
     def take(k, c, source):
+        info(2 * k + c, source, source).wait_recv()
         for j in range(2):
             slot(k, c, j, source, source).wait_recv()
             code = code_of(info_ref, source, j)
@@ -236,7 +261,7 @@
     across(0)
 
     def arrive(k):
-        pl.when(k + TILES_AHEAD <= 15)(lambda: send_tiles(k + TILES_AHEAD))
+        pl.when(k + TILES_AHEAD <= 15)(lambda: advance(k + TILES_AHEAD))
         pl.when(k + OUT_AHEAD <= 15)(lambda: outward(k + OUT_AHEAD))
         dz, dx = step_of(k)
         for c in range(2):
@@ -260,14 +285,14 @@
         )
         copy.start()
         swaps.append(copy)
-    for copy in sent:
-        copy.wait_send()
+    info(1, pair, me).wait_send()
     for j in range(2):
         slot(0, 1, j, pair, me).wait_send()
 
     def drain(k):
         plane(k, pair, me).wait_send()
         for c in range(2):
+            info(2 * k + c, pair, me).wait_send()
             for j in range(2):
                 slot(k, c, j, pair, me).wait_send()
 
@@ -288,9 +313,9 @@
     dens_ref[...] = total
 
 
-def dispatch(sel, meta, tiles, ao, occ):
+def dispatch(dest, place, rows, cols, tiles, ao, occ):
     vmem, smem = pl.BlockSpec(memory_space=pltpu.VMEM), pl.BlockSpec(memory_space=pltpu.SMEM)
-    dma = pltpu.SemaphoreType.DMA
+    dma, hbm = pltpu.SemaphoreType.DMA, pl.BlockSpec(memory_space=pltpu.HBM)
     return pl.pallas_call(
         dispatch_kernel,
         out_shape=(
@@ -298,9 +323,14 @@
             jax.ShapeDtypeStruct((2 * NWIDE,), jnp.int32),
             jax.ShapeDtypeStruct((NWIDE * SIDE, NOCC, BLK), jnp.bfloat16),
         ),
-        in_specs=[smem, vmem, vmem, vmem, vmem],
-        out_specs=(vmem, smem, pl.BlockSpec(memory_space=pltpu.HBM)),
+        in_specs=[smem, smem, smem, smem, hbm, hbm, hbm],
+        out_specs=(vmem, smem, hbm),
         scratch_shapes=[
+            pltpu.VMEM((TILES, ROWS, BLK), jnp.bfloat16),
+            pltpu.VMEM((NBAT * KB, BLK, PTS), jnp.bfloat16),
+            pltpu.VMEM((BLK, NOCC), jnp.bfloat16),
+            dma((3,)),
+            pltpu.VMEM((NWIDE, 8, BLK), jnp.int32),
             pltpu.VMEM((NWIDE, 8, BLK), jnp.int32),
             pltpu.VMEM((2 * NWIDE, ROWS, BLK), jnp.bfloat16),
             pltpu.VMEM((2 * NWIDE, ROWS, BLK), jnp.bfloat16),
@@ -319,7 +349,7 @@
         cost_estimate=pl.CostEstimate(
             flops=70_000_000_000, bytes_accessed=10_000_000, transcendentals=0
         ),
-    )(sel, meta, tiles, ao, occ)
+    )(dest, place, rows, cols, tiles, ao, occ)
 
 
 def respond_kernel(
@@ -495,11 +525,13 @@
 
         lax.fori_loop(0, last, run, 0)
 
-    load_vir(0).start()
+    order = [(row + 1 + i) % SIDE for i in range(SIDE)]
+    load_vir(order[0]).start()
     each(32, lambda c: load(1 - core, c).start())
-    for q in range(1, SIDE):
+    load_vir(order[1]).start()
+    each(32, lambda c: load(core, c).start())
+    for q in order[2:]:
         load_vir(q).start()
-    each(32, lambda c: load(core, c).start())
     pl.semaphore_wait(barrier, 1 + len(peers) + SIDE - 1)
 
     def to(axis, peer, src, dst, ssem, rsem):
@@ -520,10 +552,6 @@
         load_vir(q).wait()
         give[q] = product(1 - core, q).astype(jnp.bfloat16)
         hand(q).start()
-
-    each(32, lambda c: load(1 - core, c).wait())
-    each(SIDE, other_half)
-    each(32, lambda c: load(core, c).wait())
 
     def down(q, y):
         return to(
@@ -546,7 +574,15 @@
         for k, peer in enumerate(peers):
             over(q, k, peer).start()
 
-    each(SIDE, own_half)
+    each(32, lambda c: load(1 - core, c).wait())
+    other_half(order[0])
+    each(32, lambda c: load(core, c).wait())
+
+    def both(i):
+        pl.when(i < SIDE - 1)(lambda: other_half((row + 2 + i) % SIDE))
+        own_half((row + 1 + i) % SIDE)
+
+    each(SIDE, both)
     here = pl.ds(pl.multiple_of(chip * 16, 16), 16)
 
     total = mid[row, :, :, pl.ds(0, BLK)].astype(jnp.float32)
@@ -652,27 +688,10 @@
     occ_coef,
     vir_coef,
 ):
-    tile_count = dens_tiles.shape[0]
-    targets = tile_dest.reshape(-1)
-    routes = jnp.arange(targets.shape[0])
-    earlier = (targets[:, None] == targets[None, :]) & (routes[:, None] > routes[None, :])
-    position = targets * 2 + jnp.sum(earlier.astype(jnp.int32), axis=1)
-    place = tile_place.reshape(-1)
-    batch, slot = place // 25, place % 25
-    code = (
-        (batch * KB + slot // KB) + 16 * (batch * KB + slot % KB) + 256 * batch + 512 * place + 32768
-        + 65536 * jnp.repeat(tile_rows, 2) + 262144 * jnp.repeat(tile_cols, 2)
-    )
-    chosen = position[None, :] == jnp.arange(2 * NWIDE)[:, None]
-    sel = jnp.sum(jnp.where(chosen, routes[None, :] // 2, 0), axis=1)
-    sent = jnp.sum(jnp.where(chosen, code[None, :], 0), axis=1)
-    meta = jnp.broadcast_to(
-        jnp.pad(sent.reshape(NWIDE, 1, 2), ((0, 0), (0, 0), (0, BLK - 2))), (NWIDE, 8, BLK)
-    )
-
     ao = ao_values.reshape(NBAT * KB, BLK, PTS)
     dens, codes, occ_all = dispatch(
-        sel, meta, dens_tiles.reshape(tile_count, ROWS, BLK), ao, occ_coef
+        tile_dest.T, tile_place.T, tile_rows, tile_cols,
+        dens_tiles.reshape(TILES, ROWS, BLK), ao, occ_coef,
     )
     left = respond(
         codes, point_count, dens, weights, kernel_first, kernel_second, ao,

time: 189 us -> 180 us (0.952)
  other arithmetic: 3.51 us -> 0 us
  local copies, waits for them, and re-layouts: 3.25 us -> 0.62 us
    pallas_call x1, Pallas kernels: 37.7 us -> 30.8 us  [reduced(): pl.pallas_call(reduce_kernel, out_shape=jax.ShapeDtypeStruct((FIELDS, 16,...]
    pallas_call x1, Pallas kernels: 26.6 us -> 30.1 us  [respond(): pl.pallas_call(respond_kernel, out_shape=jax.ShapeDtypeStruct((32, 2 * HA...]
    pallas_call x1, Pallas kernels: 117 us -> 119 us  [dispatch(): pl.pallas_call(dispatch_kernel, out_shape=(jax.ShapeDtypeStruct((8, PTS),...]
where the time goes in v4:
time: 180 us
  Pallas kernels  180 us (100%)
    pallas_call x1, Pallas kernels, dispatch(): pl.pallas_call(dispatch_kernel, out_shape=(jax.ShapeDtypeStruct((8, PTS),...  119 us
    pallas_call x1, Pallas kernels, reduced(): pl.pallas_call(reduce_kernel, out_shape=jax.ShapeDtypeStruct((FIELDS, 16,...  30.8 us
    pallas_call x1, Pallas kernels, respond(): pl.pallas_call(respond_kernel, out_shape=jax.ShapeDtypeStruct((32, 2 * HA...  30.1 us

profile of v4, /device:TPU:0, one launch (start us, length us, event | category | flops | bytes accessed | tf_op | source)
XLA Modules:
  0.0 180.2 jit_solution(10756809388623376759)
XLA Ops:
  0.0 118.6 %shard_map.118 = (f32[8,1280]{1,0:T(8,128)}, s32[64]{0:T(128)}, bf16[128,512,128]{2,1,0:T(8,128)(2,1)}) custom-call(s32[2,16]{1,0:T(2,128)} %bitcast.7, s32[2,16]{1,0:T(2,128)} %bitcast.8, s32[16]{0:T(128)} %rows_ref.1, s32[16]{0:T(128)} %cols_ref.1, bf16[16,384,128]{2,1,0:T(8,128)(2,1)} %bitcast.6, bf16[10,128,1280]{2,1,0:T(8,128)(2,1)} %bitcast.4, ...), custom_call_target="tpu_custom_call" | custom-call | flops 70000001024 | bytes 10000000 | tf_op jit(solution)/shard_map/pallas_call | solution.py:319
  118.6 30.1 %shard_map.119.left_hbm = bf16[32,1536,128]{2,1,0:T(8,128)(2,1)} custom-call(s32[64]{0:T(128)} %get-tuple-element.8.code_ref, s32[2]{0:T(128)} %count_ref.1, f32[8,1280]{1,0:T(8,128)} %get-tuple-element.9.dens_ref, f32[2,1280]{1,0:T(2,128)} %weight_ref.1, f32[2,1280]{1,0:T(2,128)} %first_ref.1, f32[2,1280]{1,0:T(2,128)} %second_ref.1, ...), custom_call_target="tpu_custom_call" | custom-call | flops 30000001024 | bytes 30000000 | tf_op jit(solution)/shard_map/pallas_call | solution.py:466
  148.8 30.8 %shard_map.120 = f32[3,16,256]{2,1,0:T(8,128)S(1)} custom-call(bf16[32,1536,128]{2,1,0:T(8,128)(2,1)} %shard_map.119.left_hbm, bf16[4096,1024]{1,0:T(8,128)(2,1)} %vir_hbm.1), custom_call_target="tpu_custom_call" | custom-call | flops 30000001024 | bytes 30000000 | tf_op jit(solution)/shard_map/pallas_call | solution.py:647
  179.6 0.6 copy.14

commit v5 on v4

--- a/solution.py
+++ b/solution.py
@@ -15,11 +15,12 @@
 SIDE = 4
 NWIDE = 32
 TILES = 16
+SLOTS = 8
 ROWS = FIELDS * BLK
 HALF = FIELDS * NOCC // 2
 MESH = pl.DeviceIdType.MESH
 CHIPS = [(2, 2), (1, 1), (3, 3), (1, 3), (3, 1), (1, 2), (3, 2), (2, 1), (2, 3), (0, 2), (2, 0), (0, 1), (0, 3), (1, 0), (3, 0)]
-OUT_AHEAD, TILES_AHEAD, ON_AHEAD = 8, 6, 4
+OUT_AHEAD, TILES_AHEAD, ON_AHEAD = 11, 8, 7
 OFFSETS = [(z, x, c) for z, x in CHIPS for c in range(2)] + [(0, 0, 1)]
 
 
@@ -356,8 +357,12 @@
     code_ref, count_ref, dens_ref, weight_ref, first_ref, second_ref, ao_ref, occ_hbm,
     left_hbm, occ, pot, scaled, answer, total, left, head, follow, occ_sem, left_sem,
 ):
-    load_occ = pltpu.make_async_copy(occ_hbm, occ, occ_sem)
-    load_occ.start()
+    loads = [
+        pltpu.make_async_copy(occ_hbm.at[pl.ds(i * 8, 8)], occ.at[pl.ds(i * 8, 8)], occ_sem.at[i])
+        for i in range(16)
+    ]
+    for load in loads:
+        load.start()
 
     lane = lax.broadcasted_iota(jnp.int32, (1, PTS), 1)
     for b in range(NBAT):
@@ -404,7 +409,8 @@
         return carry
 
     lax.fori_loop(0, 2 * NWIDE, link, 0)
-    load_occ.wait()
+    for load in loads:
+        load.wait()
 
     def column_sum(c, carry):
         def term(r):
@@ -441,9 +447,9 @@
             total[...] = two(first)
 
         lax.while_loop(lambda r: r >= 0, add, after(first))
-        slot = c % 2
-
-        @pl.when(c >= 2)
+        slot = c % SLOTS
+
+        @pl.when(c >= SLOTS)
         def _():
             pltpu.make_async_copy(left.at[slot], left_hbm.at[c], left_sem.at[slot]).wait()
 
@@ -456,7 +462,7 @@
         return carry
 
     lax.fori_loop(0, 32, column_sum, 0)
-    for slot in range(2):
+    for slot in range(SLOTS):
         pltpu.make_async_copy(left.at[slot], left_hbm.at[slot], left_sem.at[slot]).wait()
 
 
@@ -474,11 +480,11 @@
             pltpu.VMEM((KB * BLK, PTS), jnp.bfloat16),
             pltpu.VMEM((50, BLK, ROWS), jnp.bfloat16),
             pltpu.VMEM((NOCC, ROWS), jnp.float32),
-            pltpu.VMEM((2, 2 * HALF, BLK), jnp.bfloat16),
+            pltpu.VMEM((SLOTS, 2 * HALF, BLK), jnp.bfloat16),
             pltpu.SMEM((32,), jnp.int32),
             pltpu.SMEM((64,), jnp.int32),
-            pltpu.SemaphoreType.DMA,
-            pltpu.SemaphoreType.DMA((2,)),
+            pltpu.SemaphoreType.DMA((16,)),
+            pltpu.SemaphoreType.DMA((SLOTS,)),
         ],
         compiler_params=pltpu.CompilerParams(vmem_limit_bytes=62 * 2**20),
         cost_estimate=pl.CostEstimate(

time: 180 us -> 173 us (0.961)
  Pallas kernels: 180 us -> 171 us
    pallas_call x1, Pallas kernels: 30.1 us -> 22.5 us  [respond(): pl.pallas_call(respond_kernel, out_shape=jax.ShapeDtypeStruct((32, 2 * HA...]
    pallas_call x1, Pallas kernels: 119 us -> 115 us  [dispatch(): pl.pallas_call(dispatch_kernel, out_shape=(jax.ShapeDtypeStruct((8, PTS),...]
    pallas_call x1, Pallas kernels: 30.8 us -> 33.7 us  [reduced(): pl.pallas_call(reduce_kernel, out_shape=jax.ShapeDtypeStruct((FIELDS, 16,...]
where the time goes in v5:
time: 173 us; the launch traced here: 172 us
  Pallas kernels  171 us (99%)
    pallas_call x1, Pallas kernels, dispatch(): pl.pallas_call(dispatch_kernel, out_shape=(jax.ShapeDtypeStruct((8, PTS),...  115 us
    pallas_call x1, Pallas kernels, reduced(): pl.pallas_call(reduce_kernel, out_shape=jax.ShapeDtypeStruct((FIELDS, 16,...  33.7 us
    pallas_call x1, Pallas kernels, respond(): pl.pallas_call(respond_kernel, out_shape=jax.ShapeDtypeStruct((32, 2 * HA...  22.5 us

profile of v5, /device:TPU:0, one launch (start us, length us, event | category | flops | bytes accessed | tf_op | source)
XLA Modules:
  0.0 172.1 jit_solution(7126418373161477651)
XLA Ops:
  0.0 115.3 %shard_map.118 = (f32[8,1280]{1,0:T(8,128)}, s32[64]{0:T(128)}, bf16[128,512,128]{2,1,0:T(8,128)(2,1)}) custom-call(s32[2,16]{1,0:T(2,128)} %bitcast.7, s32[2,16]{1,0:T(2,128)} %bitcast.8, s32[16]{0:T(128)} %rows_ref.1, s32[16]{0:T(128)} %cols_ref.1, bf16[16,384,128]{2,1,0:T(8,128)(2,1)} %bitcast.6, bf16[10,128,1280]{2,1,0:T(8,128)(2,1)} %bitcast.4, ...), custom_call_target="tpu_custom_call" | custom-call | flops 70000001024 | bytes 10000000 | tf_op jit(solution)/shard_map/pallas_call | solution.py:320
  115.3 22.5 %shard_map.119.left_hbm = bf16[32,1536,128]{2,1,0:T(8,128)(2,1)} custom-call(s32[64]{0:T(128)} %get-tuple-element.8.code_ref, s32[2]{0:T(128)} %count_ref.1, f32[8,1280]{1,0:T(8,128)} %get-tuple-element.9.dens_ref, f32[2,1280]{1,0:T(2,128)} %weight_ref.1, f32[2,1280]{1,0:T(2,128)} %first_ref.1, f32[2,1280]{1,0:T(2,128)} %second_ref.1, ...), custom_call_target="tpu_custom_call" | custom-call | flops 30000001024 | bytes 30000000 | tf_op jit(solution)/shard_map/pallas_call | solution.py:472
  137.8 33.7 %shard_map.120 = f32[3,16,256]{2,1,0:T(8,128)S(1)} custom-call(bf16[32,1536,128]{2,1,0:T(8,128)(2,1)} %shard_map.119.left_hbm, bf16[4096,1024]{1,0:T(8,128)(2,1)} %vir_hbm.1), custom_call_target="tpu_custom_call" | custom-call | flops 30000001024 | bytes 30000000 | tf_op jit(solution)/shard_map/pallas_call | solution.py:653
  171.5 0.6 copy.14

commit v6 on v5

--- a/solution.py
+++ b/solution.py
@@ -436,28 +436,37 @@
             total[...] += two(r)
             return after(r)
 
-        first = head[c]
-
-        @pl.when(first < 0)
-        def _():
-            total[...] = jnp.zeros_like(total)
-
-        @pl.when(first >= 0)
-        def _():
-            total[...] = two(first)
-
-        lax.while_loop(lambda r: r >= 0, add, after(first))
         slot = c % SLOTS
 
         @pl.when(c >= SLOTS)
         def _():
             pltpu.make_async_copy(left.at[slot], left_hbm.at[c], left_sem.at[slot]).wait()
 
-        for half in range(2):
-            for f in range(FIELDS):
-                left[slot, pl.ds(half * HALF + f * 256, 256), :] = total[
-                    half * 256 : (half + 1) * 256, f * BLK : (f + 1) * BLK
-                ].astype(jnp.bfloat16)
+        def emit(value):
+            value = value.astype(jnp.bfloat16)
+            for half in range(2):
+                for f in range(FIELDS):
+                    left[slot, pl.ds(half * HALF + f * 256, 256), :] = value[
+                        half * 256 : (half + 1) * 256, f * BLK : (f + 1) * BLK
+                    ]
+
+        first = head[c]
+        second = after(first)
+
+        @pl.when(first < 0)
+        def _():
+            left[slot] = jnp.zeros((2 * HALF, BLK), jnp.bfloat16)
+
+        @pl.when(jnp.logical_and(first >= 0, second < 0))
+        def _():
+            emit(two(first))
+
+        @pl.when(second >= 0)
+        def _():
+            total[...] = two(first)
+            lax.while_loop(lambda r: r >= 0, add, second)
+            emit(total[...])
+
         pltpu.make_async_copy(left.at[slot], left_hbm.at[c], left_sem.at[slot]).start()
         return carry
 

time: 173 us -> 172 us (level)
    pallas_call x1, Pallas kernels: 33.7 us -> 31.5 us  [reduced(): pl.pallas_call(reduce_kernel, out_shape=jax.ShapeDtypeStruct((FIELDS, 16,...]
where the time goes in v6:
time: 172 us; the launch traced here: 171 us
  Pallas kernels  170 us (99%)
    pallas_call x1, Pallas kernels, dispatch(): pl.pallas_call(dispatch_kernel, out_shape=(jax.ShapeDtypeStruct((8, PTS),...  115 us
    pallas_call x1, Pallas kernels, reduced(): pl.pallas_call(reduce_kernel, out_shape=jax.ShapeDtypeStruct((FIELDS, 16,...  31.5 us
    pallas_call x1, Pallas kernels, respond(): pl.pallas_call(respond_kernel, out_shape=jax.ShapeDtypeStruct((32, 2 * HA...  23.1 us

profile of v6, /device:TPU:0, one launch (start us, length us, event | category | flops | bytes accessed | tf_op | source)
XLA Modules:
  0.0 170.6 jit_solution(284710080037440340)
XLA Ops:
  0.0 115.3 %shard_map.118 = (f32[8,1280]{1,0:T(8,128)}, s32[64]{0:T(128)}, bf16[128,512,128]{2,1,0:T(8,128)(2,1)}) custom-call(s32[2,16]{1,0:T(2,128)} %bitcast.7, s32[2,16]{1,0:T(2,128)} %bitcast.8, s32[16]{0:T(128)} %rows_ref.1, s32[16]{0:T(128)} %cols_ref.1, bf16[16,384,128]{2,1,0:T(8,128)(2,1)} %bitcast.6, bf16[10,128,1280]{2,1,0:T(8,128)(2,1)} %bitcast.4, ...), custom_call_target="tpu_custom_call" | custom-call | flops 70000001024 | bytes 10000000 | tf_op jit(solution)/shard_map/pallas_call | solution.py:320
  115.3 23.1 %shard_map.119.left_hbm = bf16[32,1536,128]{2,1,0:T(8,128)(2,1)} custom-call(s32[64]{0:T(128)} %get-tuple-element.8.code_ref, s32[2]{0:T(128)} %count_ref.1, f32[8,1280]{1,0:T(8,128)} %get-tuple-element.9.dens_ref, f32[2,1280]{1,0:T(2,128)} %weight_ref.1, f32[2,1280]{1,0:T(2,128)} %first_ref.1, f32[2,1280]{1,0:T(2,128)} %second_ref.1, ...), custom_call_target="tpu_custom_call" | custom-call | flops 30000001024 | bytes 30000000 | tf_op jit(solution)/shard_map/pallas_call | solution.py:481
  138.5 31.5 %shard_map.120 = f32[3,16,256]{2,1,0:T(8,128)S(1)} custom-call(bf16[32,1536,128]{2,1,0:T(8,128)(2,1)} %shard_map.119.left_hbm, bf16[4096,1024]{1,0:T(8,128)(2,1)} %vir_hbm.1), custom_call_target="tpu_custom_call" | custom-call | flops 30000001024 | bytes 30000000 | tf_op jit(solution)/shard_map/pallas_call | solution.py:662
  170.0 0.6 copy.14
